TPU v7x, 32 devices: a whole 2x2x4 slice. The times are simulated.
32 devices in a mesh: aa: 2 (over core), ba: 16 (over z, y, x).
Axes of the slice: x: 2, y: 2, z: 4, core: 2. Of those that a mesh axis runs over, the one named last changes fastest.
Arguments:
- queries: bfloat16 [2, 16, 192, 1024], P('aa', 'ba'), may hold values from -6 to 6
- key_rows: bfloat16 [2, 16, 192, 1024], P('aa', 'ba'), may hold values from -6 to 6
- value_rows: bfloat16 [2, 16, 192, 1024], P('aa', 'ba'), may hold values from -6 to 6
- out_proj: bfloat16 [2, 1024, 1024], P('aa', 'ba'), may hold values from -0.1875 to 0.1875
- scale_ids: int32 [16, 192], P('ba'), may hold values from 0 to 7, never falling along the last dimension, each value on 1 to 64 neighbouring positions
- residual_in: bfloat16 [16, 192, 1024], P('ba'), may hold values from -4 to 4
- cotangent: bfloat16 [16, 192, 1024], P('ba'), may hold values from -6 to 6
Outputs:
- residual_out: bfloat16 [2, 16, 192, 1024], P('aa', 'ba')
- grad_query: bfloat16 [2, 16, 192, 1024], P('aa', 'ba')
- grad_key: bfloat16 [2, 16, 192, 1024], P('aa', 'ba')
- grad_value: bfloat16 [2, 16, 192, 1024], P('aa', 'ba')
- grad_proj: float32 [2, 1024, 1024], P('aa', 'ba')
Inputs may be any that keep to these rules, and one draw needn't show every extreme that they name: `scale_ids`: for each image the scale ids never fall along the tokens; every scale from 0 to 7 is present, with 1 to 64 tokens.
All inputs are finite; a program needn't handle non-finite values.
Results may differ from a plain program's by a relative error of at most 0.0086.
Values may be sent and summed in bfloat16 or wider, within the bound.
No kernel may reach another device: no remote copies, remote signals or barrier semaphores. Data moves between devices by JAX's collectives and lax.ppermute only.
A program may use at most 64 MiB of HBM per device.

v0:
```python
import jax
import jax.numpy as jnp
from jax import lax
from jax.sharding import PartitionSpec as P

HD = 64


def passed_along(value, axis, by):
    devices = lax.axis_size(axis)
    pairs = [(i, i + by) for i in range(devices) if 0 <= i + by < devices]
    return lax.ppermute(value, axis, pairs)


def local(queries, key_rows, value_rows, out_proj, scale_ids, residual_in, cotangent):
    images = queries.shape[1]
    length = queries.shape[2]
    inner_width = queries.shape[3]
    head_count = inner_width // HD
    res_width = residual_in.shape[2]
    flat_rows = images * length
    score_scale = HD ** (-0.5)
    image_weight = 1.0 / (lax.axis_size("ba") * images)
    w_full = lax.all_gather(out_proj, "ba", axis=1, tiled=True)[0]
    visible = scale_ids[:, None, :] <= scale_ids[:, :, None]
    q_heads = queries[0].reshape(images, length, head_count, HD)
    k_heads = key_rows[0].reshape(images, length, head_count, HD)
    v_heads = value_rows[0].reshape(images, length, head_count, HD)
    scores = (
        jnp.einsum("bihd,bjhd->bhij", q_heads, k_heads, preferred_element_type=jnp.float32)
        * score_scale
    )
    scores = jnp.where(visible[:, None], scores, -jnp.inf)
    row_max = jnp.max(scores, axis=-1, keepdims=True)
    lifted = jnp.exp(scores - row_max)
    attn_probs = lifted / jnp.sum(lifted, axis=-1, keepdims=True)
    probs_low = attn_probs.astype(jnp.bfloat16)
    attended = jnp.einsum("bhij,bjhd->bihd", probs_low, v_heads, preferred_element_type=jnp.float32)
    attn_rows = attended.astype(jnp.bfloat16).reshape(flat_rows, inner_width)
    branch = jnp.dot(attn_rows, w_full, preferred_element_type=jnp.float32)

    def relay_step(hop_index, running):
        return branch + passed_along(running, "aa", 1)

    carried = lax.fori_loop(0, lax.axis_size("aa") - 1, relay_step, branch)
    residual_rows = residual_in.reshape(flat_rows, res_width).astype(jnp.float32) + carried
    residual_out = residual_rows.astype(jnp.bfloat16).reshape(images, length, res_width)
    cot_rows = cotangent.reshape(flat_rows, res_width)
    d_attn = lax.dot_general(
        cot_rows, w_full, (((1,), (1,)), ((), ())), preferred_element_type=jnp.float32
    ).astype(jnp.bfloat16)
    product = lax.dot_general(
        attn_rows, cot_rows, (((0,), (0,)), ((), ())), preferred_element_type=jnp.float32
    )
    grad_proj = lax.psum_scatter(product * image_weight, "ba", scatter_dimension=0, tiled=True)
    d_heads = d_attn.reshape(images, length, head_count, HD)
    grad_value = jnp.einsum(
        "bhij,bihd->bjhd", probs_low, d_heads, preferred_element_type=jnp.float32
    )
    d_probs = jnp.einsum("bihd,bjhd->bhij", d_heads, v_heads, preferred_element_type=jnp.float32)
    row_delta = jnp.sum(attn_probs * d_probs, axis=-1, keepdims=True)
    d_scores = (attn_probs * (d_probs - row_delta) * score_scale).astype(jnp.bfloat16)
    grad_query = jnp.einsum(
        "bhij,bjhd->bihd", d_scores, k_heads, preferred_element_type=jnp.float32
    )
    grad_key = jnp.einsum("bhij,bihd->bjhd", d_scores, q_heads, preferred_element_type=jnp.float32)
    return (
        residual_out[None],
        grad_query.reshape(images, length, inner_width).astype(jnp.bfloat16)[None],
        grad_key.reshape(images, length, inner_width).astype(jnp.bfloat16)[None],
        grad_value.reshape(images, length, inner_width).astype(jnp.bfloat16)[None],
        grad_proj[None],
    )


def solution(mesh):
    placed = (
        P("aa", "ba", None, None),
        P("aa", "ba", None, None),
        P("aa", "ba", None, None),
        P("aa", "ba", None),
        P("ba", None),
        P("ba", None, None),
        P("ba", None, None),
    )
    return jax.shard_map(
        local,
        mesh=mesh,
        in_specs=placed,
        out_specs=(
            P("aa", "ba", None, None),
            P("aa", "ba", None, None),
            P("aa", "ba", None, None),
            P("aa", "ba", None, None),
            P("aa", "ba", None),
        ),
        check_vma=False,
    )
```

profile of v0, /device:TPU:0, one launch (start us, length us, event | category | flops | bytes accessed | tf_op | source)
XLA Modules:
  0.0 177.7 jit_solution(12900894556805366626)
XLA Ops:
  7.2 0.0 copy-start
  7.2 0.0 all-gather.2.cloned.1.call-start
  7.2 0.7 all-gather.2.cloned.1.call-update
  7.9 0.0 reduce-scatter.2.cloned.1.call-start
  8.0 1.2 copy.27
  9.2 0.0 copy-start.4
  9.2 1.4 copy.28
  10.6 0.0 copy-start.2
  10.6 1.4 copy.29
  12.0 0.8 broadcast_compare_fusion
  12.8 2.9 %fusion.44 = (f32[16,192]{1,0:T(8,128)S(1)}, f32[16,192,192]{1,2,0:T(8,128)}) fusion(pred[192,192]{0,1:T(8,128)(4,1)S(1)} %broadcast_compare_fusion, bf16[192,16,64]{0,2,1:T(8,128)(2,1)S(1)} %bitcast.69, bf16[192,16,64]{0,2,1:T(8,128)(2,1)S(1)} %bitcast.67), kind=kOutput, calls=%fused_computation.41 | convolution fusion | flops 77856960 | bytes 3194880 | tf_op jit(solution)/shard_map/sub | solution.py:35
  15.8 0.0 copy-done.4
  15.8 0.0 copy-done.2
  15.8 2.3 %convolution_convert_fusion = bf16[16,192,64]{1,2,0:T(8,128)(2,1)S(1)} fusion(bf16[192,16,64]{0,2,1:T(8,128)(2,1)S(1)} %bitcast.63, f32[16,192,192]{1,2,0:T(8,128)} %get-tuple-element.25, f32[16,192]{1,0:T(8,128)S(1)} %get-tuple-element.24), kind=kOutput, calls=%fused_computation.23 | convolution fusion | flops 76873728 | bytes 3158016 | tf_op jit(solution)/shard_map/bhij,bjhd->bihd/dot_general | solution.py:38
  18.1 0.0 copy-done
  18.1 2.6 %convolution_multiply_fusion = f32[1024,1024]{1,0:T(8,128)} fusion(bf16[192,1024]{0,1:T(8,128)(2,1)S(1)} %bitcast.61, bf16[1,192,1024]{2,1,0:T(8,128)(2,1)S(1)} %copy-done), kind=kOutput, calls=%fused_computation.8 | convolution fusion | flops 403701760 | bytes 4980736 | tf_op jit(solution)/shard_map/dot_general | solution.py:52
  20.7 0.0 reduce-scatter.2.cloned.1.call-update
  20.8 53.1 %all-gather.2.cloned.1.call-done = bf16[1,1024,1024]{2,1,0:T(8,128)(2,1)} async-done(((bf16[1,64,1024]{2,1,0:T(8,128)(2,1)}), bf16[1,1024,1024]{2,1,0:T(8,128)(2,1)}) %all-gather.2.cloned.1.call-update) | async-done | bytes 2097168 | tf_op jit(solution)/shard_map/all_gather | solution.py:24
  73.9 0.0 copy-start.1
  73.9 2.3 %fusion.8 = f32[192,1024]{1,0:T(8,128)S(1)} fusion(bf16[192,1024]{0,1:T(8,128)(2,1)S(1)} %bitcast.62, bf16[1,1024,1024]{2,1,0:T(8,128)(2,1)} %all-gather.2.cloned.1.call-done), kind=kOutput, calls=%fused_computation.11 | convolution fusion | flops 402653184 | bytes 3276800 | tf_op jit(solution)/shard_map/dot_general | solution.py:40
  76.2 1.3 collective-permute-start
  77.6 0.0 copy-done.1
  77.6 0.9 fusion.27
  78.5 0.2 copy.31
  78.7 0.0 copy-start.5
  78.7 2.3 %fusion.45 = f32[16,192,192]{1,2,0:T(8,128)} fusion(bf16[192,16,64]{0,2,1:T(8,128)(2,1)S(1)} %bitcast.65, bf16[192,16,64]{0,2,1:T(8,128)(2,1)S(1)} %bitcast.64), kind=kOutput, calls=%fused_computation.42 | convolution fusion | flops 75497472 | bytes 3145728 | tf_op jit(solution)/shard_map/bihd,bjhd->bhij/dot_general | solution.py:60
  81.0 0.0 copy-done.5
  81.0 0.0 copy-start.3
  81.0 6.6 %fusion.24 = bf16[16,192,64]{1,2,0:T(8,128)(2,1)} fusion(bf16[192,16,64]{0,2,1:T(8,128)(2,1)S(1)} %bitcast.70, f32[16,192,192]{1,2,0:T(8,128)} %fusion.45, f32[16,192,192]{1,2,0:T(8,128)} %get-tuple-element.25, f32[16,192]{1,0:T(8,128)S(1)} %get-tuple-element.24), kind=kOutput, calls=%fused_computation.22 | convolution fusion | flops 79826112 | bytes 5517312 | tf_op jit(solution)/shard_map/bhij,bihd->bjhd/dot_general | solution.py:66
  87.7 2.0 %copy.36 = bf16[1,1,192,1024]{3,2,1,0:T(8,128)(2,1)} copy(bf16[1,1,192,1024]{2,3,1,0:T(8,128)(2,1)} %bitcast.73) | data formatting | bytes 786432
  89.6 0.0 copy-done.3
  89.6 5.8 %fusion.21 = bf16[16,192,64]{1,2,0:T(8,128)(2,1)S(1)} fusion(bf16[192,16,64]{0,2,1:T(8,128)(2,1)S(1)} %bitcast.68, f32[16,192,192]{1,2,0:T(8,128)} %fusion.45, f32[16,192,192]{1,2,0:T(8,128)} %get-tuple-element.25, f32[16,192]{1,0:T(8,128)S(1)} %get-tuple-element.24), kind=kOutput, calls=%fused_computation.21 | convolution fusion | flops 79826112 | bytes 5517312 | tf_op jit(solution)/shard_map/bhij,bjhd->bihd/dot_general | solution.py:63
  95.5 0.9 copy.35
  96.4 0.0 copy-start.6
  96.4 2.6 %convolution_convert_fusion.1 = bf16[16,64,192]{2,1,0:T(8,128)(2,1)S(1)} fusion(bf16[192,16,64]{0,2,1:T(8,128)(2,1)S(1)} %bitcast.66, f32[16,192,192]{1,2,0:T(8,128)} %get-tuple-element.25, f32[16,192]{1,0:T(8,128)S(1)} %get-tuple-element.24), kind=kOutput, calls=%fused_computation.24 | convolution fusion | flops 76873728 | bytes 3158016 | tf_op jit(solution)/shard_map/bhij,bihd->bjhd/dot_general | solution.py:57
  99.0 0.9 copy.37
  99.9 0.0 collective-permute-done
  99.9 0.0 copy-done.6
  99.9 0.9 fusion.33
  100.9 69.9 %reduce-scatter.2.cloned.1.call-done = f32[64,1024]{1,0:T(8,128)} async-done(((f32[1024,1024]{1,0:T(8,128)}), f32[64,1024]{1,0:T(8,128)}) %reduce-scatter.2.cloned.1.call-update) | async-done | bytes 262160 | tf_op jit(solution)/shard_map/reduce_scatter | solution.py:55
Async XLA Ops:
  7.2 10.9 %copy-start = (bf16[1,192,1024]{2,1,0:T(8,128)(2,1)S(1)}, bf16[1,192,1024]{2,1,0:T(8,128)(2,1)}, u32[]{:S(2)}) copy-start(bf16[1,192,1024]{2,1,0:T(8,128)(2,1)} %param.13) | copy-start | bytes 1179652
  7.2 66.7 %all-gather.2.cloned.1.call-start = ((), (), s32[]{:S(2)}) async-start(), calls=%async_computation.1 | async-start | bytes 2228224 | tf_op jit(solution)/shard_map/all_gather | solution.py:24
  7.9 162.9 %reduce-scatter.2.cloned.1.call-start = ((), (), s32[]{:S(2)}) async-start(), calls=%async_computation.2 | async-start | bytes 4456448 | tf_op jit(solution)/shard_map/reduce_scatter | solution.py:55
  9.2 6.6 %copy-start.4 = (bf16[1,1,192,1024]{2,3,1,0:T(8,128)(2,1)}, bf16[1,1,192,1024]{2,3,1,0:T(8,128)(2,1)S(1)}, u32[]{:S(2)}) copy-start(bf16[1,1,192,1024]{2,3,1,0:T(8,128)(2,1)S(1)} %copy.27) | copy-start | bytes 1179652
  10.6 5.2 %copy-start.2 = (bf16[1,1,192,1024]{2,3,1,0:T(8,128)(2,1)}, bf16[1,1,192,1024]{2,3,1,0:T(8,128)(2,1)S(1)}, u32[]{:S(2)}) copy-start(bf16[1,1,192,1024]{2,3,1,0:T(8,128)(2,1)S(1)} %copy.28) | copy-start | bytes 1179652
  73.9 3.7 %copy-start.1 = (bf16[1,1024,1024]{2,1,0:T(8,128)(2,1)S(1)}, bf16[1,1024,1024]{2,1,0:T(8,128)(2,1)}, u32[]{:S(2)}) copy-start(bf16[1,1024,1024]{2,1,0:T(8,128)(2,1)} %all-gather.2.cloned.1.call-done) | copy-start | bytes 6291460
  76.2 23.7 %collective-permute-start = (f32[192,1024]{1,0:T(8,128)S(1)}, f32[192,1024]{1,0:T(8,128)S(1)}, u32[]{:S(2)}, u32[]{:S(2)}) collective-permute-start(f32[192,1024]{1,0:T(8,128)S(1)} %fusion.8), channel_id=1, source_target_pairs={{0,16},{1,17},{2,18},{3,19},{4,20},{5,21},{6,22},{7,23},{8,24},{9,... | collective-permute-start | bytes 2359304 | tf_op jit(solution)/shard_map/while/body/eval_jaxpr/ppermute | solution.py:12
  78.7 2.4 %copy-start.5 = (bf16[1,1,192,1024]{2,3,1,0:T(8,128)(2,1)S(1)}, bf16[1,1,192,1024]{2,3,1,0:T(8,128)(2,1)}, u32[]{:S(2)}) copy-start(bf16[1,1,192,1024]{2,3,1,0:T(8,128)(2,1)} %copy-done.4) | copy-start | bytes 1179652
  81.0 8.6 %copy-start.3 = (bf16[1,1,192,1024]{2,3,1,0:T(8,128)(2,1)S(1)}, bf16[1,1,192,1024]{2,3,1,0:T(8,128)(2,1)}, u32[]{:S(2)}) copy-start(bf16[1,1,192,1024]{2,3,1,0:T(8,128)(2,1)} %copy-done.2) | copy-start | bytes 1179652
  96.4 3.5 %copy-start.6 = (bf16[1,192,1024]{2,1,0:T(8,128)(2,1)S(1)}, bf16[1,192,1024]{2,1,0:T(8,128)(2,1)}, u32[]{:S(2)}) copy-start(bf16[1,192,1024]{2,1,0:T(8,128)(2,1)} %param.12) | copy-start | bytes 1179652
Sparse Core Ops, SparseCore 0:
  10.8 63.0 all-gather.1
  76.8 94.0 reduce-scatter.1
where the time goes:
time: 178 us
  waiting for transfers between devices  124 us (70%)
  matrix products  28.5 us (16%)
  between operations  14.2 us (8%)
  local copies, waits for them, and re-layouts  8.07 us (5%)
  other arithmetic  1.78 us (1%)
    reduce_scatter x1, waiting for transfers between devices, local(): lax.psum_scatter(product * image_weight, 'ba', scatter_dimension=0, tiled...  69.9 us
    all_gather x1, waiting for transfers between devices, local(): w_full = lax.all_gather(out_proj, 'ba', axis=1, tiled=True)[0]  53.1 us
    unnamed x20, local copies, waits for them, and re-layouts  7.87 us
    dot_general x1, matrix products, local(): jnp.einsum('bhij,bihd->bjhd', d_scores, q_heads, preferred_element_type=j...  6.62 us
    dot_general x1, matrix products, local(): jnp.einsum('bhij,bjhd->bihd', d_scores, k_heads, preferred_element_type=j...  5.82 us
  transfers between devices with their start and end apart: 3, of which 2 were waited for; matrix products, arithmetic and copies ran while one was open for 22% of the time, Pallas kernels for 0%

commit v1 on v0

v1 whole, which is shorter than its diff:
```python
import functools

import jax
import jax.numpy as jnp
from jax import lax
from jax.experimental import pallas as pl
from jax.experimental.pallas import tpu as pltpu
from jax.sharding import PartitionSpec as P


HD = 64
LANES = 128


VMEM = pl.BlockSpec(memory_space=pltpu.VMEM)
HBM = pl.BlockSpec(memory_space=pltpu.HBM)
NT = (((1,), (1,)), ((), ()))
TN = (((0,), (0,)), ((), ()))
LIMIT = 54656 << 10
F32 = jnp.float32
BF16 = jnp.bfloat16


def mul(a, b, dims):
    return lax.dot_general(a, b, dims, preferred_element_type=F32)


def nn(a, b):
    return jnp.dot(a, b, preferred_element_type=F32)


def tile(index):
    return pl.ds(pl.multiple_of(index * LANES, LANES), LANES)


def place_of(bits):
    index = lax.axis_index("ba")
    return (index >> bits) & 1, (index >> (bits - 1)) & 1, index >> (bits + 1)


def first_head(shape):
    return lax.broadcasted_iota(jnp.int32, shape, 1) < HD


def forward_body(bits, ids_hbm, q_hbm, k_hbm, v_hbm, mine, others, probs_hbm, ids_ref, q_ref, k_ref, v_ref, probs, arrived, left_for):
    own, _, _ = place_of(bits)
    length, inner = q_ref.shape
    pairs = inner // LANES
    bounds = (0, pairs // 8, pairs // 2, pairs)
    ids_copy = pltpu.make_async_copy(ids_hbm, ids_ref, arrived.at[3, 0])
    ids_copy.start()

    def copies(part):
        cols = pl.ds(bounds[part] * LANES, (bounds[part + 1] - bounds[part]) * LANES)
        return [
            pltpu.make_async_copy(source.at[:, cols], target.at[:, cols], arrived.at[kind, part])
            for kind, (source, target) in enumerate(((q_hbm, q_ref), (k_hbm, k_ref), (v_hbm, v_ref)))
        ]

    for part in range(3):
        for copy in copies(part):
            copy.start()
    ids_copy.wait()
    ids = jnp.broadcast_to(ids_ref[...].astype(F32), (8, length))
    visible = jnp.transpose(ids)[:, :1] <= ids[:1]
    left = first_head((length, LANES))
    stores = []
    even = None
    for part in range(3):
        for copy in copies(part):
            copy.wait()
        for pair in range(bounds[part], bounds[part + 1]):
            cols = pl.ds(pair * LANES, LANES)
            q_pair = q_ref[:, cols] * (HD**-0.5)
            k_pair = k_ref[:, cols]
            v_pair = v_ref[:, cols]
            halves = []
            for half in range(2):
                k_head = jnp.where(left == (half == 0), k_pair, jnp.zeros_like(k_pair))
                scores = jnp.where(visible, mul(k_head, q_pair, NT), -jnp.inf)
                lifted = jnp.exp(scores - jnp.max(scores, axis=0, keepdims=True))
                low = (lifted * (1.0 / jnp.sum(lifted, axis=0, keepdims=True))).astype(BF16)
                probs[2 * pair + half] = low
                halves.append(mul(low, v_pair, TN))
            heads = pl.ds(2 * pair, 2)
            stores.append(pltpu.make_async_copy(probs.at[heads], probs_hbm.at[heads], left_for.at[pair]))
            stores[-1].start()
            rows = jnp.where(left, halves[0], halves[1]).astype(BF16)
            if pair % 2 == 0:
                even = rows
            else:
                cols = pl.ds((pair // 2) * LANES, LANES)
                mine[:, cols] = jnp.where(own == 0, even, rows)
                others[:, cols] = jnp.where(own == 0, rows, even)
    for store in stores:
        store.wait()


def backward_pair(pair, refs, low_pair, d_pair, grads, block):
    q_ref, k_ref, v_ref = refs
    cols = tile(pair)
    left = first_head(d_pair.shape)
    q_pair = q_ref[:, cols] * (HD**-0.5)
    k_pair = k_ref[:, cols] * (HD**-0.5)
    v_pair = v_ref[:, cols]
    got = []
    for half, low in enumerate(low_pair):
        wide = low.astype(F32)
        v_head = jnp.where(left == (half == 0), v_pair, jnp.zeros_like(v_pair))
        d_probs = mul(v_head, d_pair, NT)
        delta = jnp.sum(wide * d_probs, axis=0, keepdims=True)
        d_scores = (wide * (d_probs - delta)).astype(BF16)
        got.append((mul(d_scores, k_pair, TN), nn(d_scores, q_pair), nn(low, d_pair)))
    for index, (one, two) in enumerate(zip(*got)):
        grads[index, :, block] = jnp.where(left, one, two).astype(BF16)


def backward_body(bits, shift, q_ref, k_ref, v_ref, probs, d_ref, *rest):
    outs, (grads, sems) = rest[-5:-2], rest[-2:]
    kind = place_of(bits)[0] ^ shift
    stores = []
    for step in range(sems.shape[1]):
        pair = 2 * step + kind
        block = pl.ds(step * LANES, LANES)
        if shift == 0:
            d_pair = mul(d_ref[...], rest[0][block, :], NT).astype(BF16)
        else:
            d_pair = d_ref[:, block]
        backward_pair(pair, (q_ref, k_ref, v_ref), (probs[2 * pair], probs[2 * pair + 1]), d_pair, grads, block)
        for index, out in enumerate(outs):
            stores.append(pltpu.make_async_copy(grads.at[index, :, block], out.at[:, tile(pair)], sems.at[index, step]))
            stores[-1].start()
    for store in stores:
        store.wait()


def product_body(bits, distances, weight, a_own, a_mate, c_own, c_mate, keep, send):
    _, upper, top = place_of(bits)
    for step, distance in enumerate(distances):
        cols = tile(jnp.bitwise_xor(top, distance))
        rows = mul(a_own[:, cols], c_own[...], TN) + mul(a_mate[:, cols], c_mate[...], TN)
        rows = rows * weight
        low, high = rows[:HD], rows[HD:]
        keep[step] = jnp.where(upper == 0, low, high)
        send[step] = jnp.where(upper == 0, high, low).astype(BF16)


def weights_body(bits, near, near_x, far, far_x, a_own, a_mate, c_mate, d_mate, branches, w_out):
    _, upper, top = place_of(bits)
    half = near.shape[0]
    for distance in range(2 * half):
        mine, other = (far, far_x) if distance % 2 else (near, near_x)
        base = jnp.bitwise_xor(top, distance) * LANES
        step = distance // 2
        w_out[pl.ds(pl.multiple_of(base + upper * HD, HD), HD), :] = mine[step]
        w_out[pl.ds(pl.multiple_of(base + (1 - upper) * HD, HD), HD), :] = other[step]
    res = w_out.shape[1]
    d_mate[...] = mul(c_mate[...], w_out[...], NT).astype(BF16)
    branches[:, :res] = nn(a_own[...], w_out[...]).astype(BF16)
    branches[:, res:] = nn(a_mate[...], w_out[...]).astype(BF16)


def step(queries, key_rows, value_rows, out_proj, scale_ids, residual_in, cotangent):
    images, length, inner = queries.shape[1:]
    res = residual_in.shape[2]
    n = lax.axis_size("ba")
    sections = lax.axis_size("aa")
    block = out_proj.shape[1]
    tiles = inner // (2 * LANES)
    bits = (LANES // block).bit_length() - 1
    assert images == 1 and block << bits == LANES and bits > 0 and n == tiles << (bits + 1) and tiles & (tiles - 1) == 0
    weight = 1.0 / (n * images)

    def swap(value, by):
        return lax.ppermute(value, "ba", [(i, i ^ by) for i in range(n)])

    def kernel(body, outs, flops, *given, hbm=0, out_specs=None, aliases={}, scratch=(), limit=24 << 20):
        return pl.pallas_call(
            body,
            out_shape=outs,
            in_specs=[VMEM] * (len(given) - hbm) + [HBM] * hbm,
            out_specs=out_specs or jax.tree.map(lambda _: VMEM, outs),
            input_output_aliases=aliases,
            scratch_shapes=scratch,
            compiler_params=pltpu.CompilerParams(vmem_limit_bytes=limit),
            cost_estimate=pl.CostEstimate(flops=flops, bytes_accessed=1 << 20, transcendentals=0),
        )(*given)

    def shaped(dtype, *dims):
        return jax.ShapeDtypeStruct(dims, dtype)

    index = lax.axis_index("ba")
    mate = 1 << bits
    side = 1 << (bits - 1)
    half = tiles // 2
    levels = tiles.bit_length() - 1
    width = inner // 2

    q, k, v = queries[0, 0], key_rows[0, 0], value_rows[0, 0]
    c_own = cotangent[0]

    c_mate = swap(c_own, mate)
    pairs = [(i, i + 1) for i in range(sections - 1)]
    near = out_proj
    for bit in reversed(range(1, levels)):
        near = jnp.stack([near, swap(near, mate << (bit + 1))], axis=1)
        near = near.reshape(-1, *out_proj.shape[1:])
    for bit in range(bits - 1):
        other = swap(near, 1 << bit)
        odd = ((index >> bit) & 1) == 1
        near = jnp.concatenate([jnp.where(odd, other, near), jnp.where(odd, near, other)], axis=1)
    far = swap(near, mate << 1)
    near_x = swap(near, side)

    far_x = swap(near_x, mate << 1)

    a_own, a_sent, probs = kernel(
        functools.partial(forward_body, bits),
        (shaped(BF16, length, width), shaped(BF16, length, width), shaped(BF16, inner // HD, length, length)),
        16 * length * length * inner,
        scale_ids, q, k, v,
        hbm=4,
        out_specs=(VMEM, VMEM, HBM),
        limit=LIMIT,
        scratch=[pltpu.VMEM((1, length), jnp.int32)]
        + [pltpu.VMEM((length, inner), BF16)] * 3
        + [pltpu.VMEM((inner // HD, length, length), BF16)]
        + [pltpu.SemaphoreType.DMA((4, 3)), pltpu.SemaphoreType.DMA((inner // LANES,))],
    )
    a_mate = swap(a_sent, mate)

    def product(distances):
        keep, send = kernel(
            functools.partial(product_body, bits, distances, weight),
            (shaped(F32, half, HD, res), shaped(BF16, half, HD, res)),
            4 * length * half * LANES * res,
            a_own, a_mate, c_own, c_mate,
        )
        total = keep + swap(send, side).astype(F32)
        for bit in reversed(range(bits - 1)):
            odd = ((index >> bit) & 1) == 1
            low, high = jnp.split(total, 2, axis=1)
            sent = jnp.where(odd, low, high).astype(BF16)
            total = jnp.where(odd, high, low) + swap(sent, 1 << bit).astype(F32)
        return total

    far_sum = product(range(1, tiles, 2))
    near_sum = product(range(0, tiles, 2))
    sums = near_sum + swap(far_sum.astype(BF16), mate << 1).astype(F32)
    for bit in range(1, levels):
        kept, sent = sums[0::2], sums[1::2]
        sums = kept + swap(sent.astype(BF16), mate << (bit + 1)).astype(F32)
    grad_proj = sums[0]

    d_mate, branches, w_half = kernel(
        functools.partial(weights_body, bits),
        (shaped(BF16, length, width), shaped(BF16, length, 2 * res), shaped(BF16, width, res)),
        6 * length * width * res,
        near, near_x, far, far_x, a_own, a_mate, c_mate,
    )
    d_got = swap(d_mate, mate)
    carried = branches
    for _ in range(sections - 1):
        passed = lax.ppermute(carried, "aa", pairs)
        carried = (branches.astype(F32) + passed.astype(F32)).astype(BF16)
    other = swap(carried[:, res:], mate)
    total = residual_in[0].astype(F32) + carried[:, :res].astype(F32) + other.astype(F32)
    residual_out = total.astype(BF16)

    grads = ()
    for shift, d_rows, rows in ((0, c_own, (w_half,)), (1, d_got, ())):
        grads = kernel(
            functools.partial(backward_body, bits, shift),
            (shaped(BF16, length, inner),) * 3,
            16 * length * length * inner,
            q, k, v, probs, d_rows, *rows, *grads,
            hbm=len(grads),
            out_specs=(HBM,) * 3,
            aliases={5 + i: i for i in range(len(grads))},
            scratch=[pltpu.VMEM((3, length, width), BF16), pltpu.SemaphoreType.DMA((3, tiles))],
        )
    grad_q, grad_k, grad_v = grads
    return (
        residual_out[None, None],
        grad_q[None, None],
        grad_k[None, None],
        grad_v[None, None],
        grad_proj[None],
    )


def solution(mesh):
    placed = (
        P("aa", "ba", None, None),
        P("aa", "ba", None, None),
        P("aa", "ba", None, None),
        P("aa", "ba", None),
        P("ba", None),
        P("ba", None, None),
        P("ba", None, None),
    )
    return jax.shard_map(
        step,
        mesh=mesh,
        in_specs=placed,
        out_specs=(
            P("aa", "ba", None, None),
            P("aa", "ba", None, None),
            P("aa", "ba", None, None),
            P("aa", "ba", None, None),
            P("aa", "ba", None),
        ),
        check_vma=False,
    )
```

time: 178 us -> 62.4 us (0.35)
  waiting for transfers between devices: 124 us -> 26 us
  matrix products: 28.5 us -> 0 us
  starting transfers between devices: 1.42 us -> 18.9 us
  between operations: 14.2 us -> 0.81 us
  Pallas kernels: 0 us -> 12.8 us
  local copies, waits for them, and re-layouts: 8.07 us -> 0.75 us
    reduce_scatter x1 -> x0, waiting for transfers between devices: 69.9 us -> none  [local(): lax.psum_scatter(product * image_weight, 'ba', scatter_dimension=0, tiled...]
    all_gather x1 -> x0, waiting for transfers between devices: 53.1 us -> none  [local(): w_full = lax.all_gather(out_proj, 'ba', axis=1, tiled=True)[0]]
    ppermute x1 -> x13, waiting for transfers between devices: 0.01 us -> 26 us  [the longest x12 26 us: swap(): return lax.ppermute(value, 'ba', [(i, i ^ by) for i in range(n)])]
    dot_general x8 -> x0, matrix products: 25.5 us -> none  [the longest x1 6.62 us: local(): jnp.einsum('bhij,bihd->bjhd', d_scores, q_heads, preferred_element_type=j...]
    ppermute x1 -> x13, starting transfers between devices: 1.34 us -> 18.9 us  [the longest x12 17.5 us: swap(): return lax.ppermute(value, 'ba', [(i, i ^ by) for i in range(n)])]
    pallas_call x0 -> x6, Pallas kernels: none -> 12.8 us  [kernel(): pl.pallas_call(body, out_shape=outs, in_specs=[VMEM] * (len(given) - hbm)...]
    unnamed x20 -> x14, local copies, waits for them, and re-layouts: 7.87 us -> 0.71 us
    sub x1 -> x0, matrix products: 2.94 us -> none  [local(): lifted = jnp.exp(scores - row_max)]
  transfers between devices with their start and end apart: 3 -> 13, of which waited for: 2 -> 6; matrix products, arithmetic and copies ran while one was open for 22% -> 2% of each run, Pallas kernels for 0% -> 19%
where the time goes in v1:
time: 62.4 us; the launch traced here: 62.2 us
  waiting for transfers between devices  26 us (42%)
  starting transfers between devices  18.9 us (30%)
  Pallas kernels  12.8 us (21%)
  other arithmetic  3 us (5%)
  between operations  0.81 us (1%)
  local copies, waits for them, and re-layouts  0.75 us (1%)
    ppermute x12, waiting for transfers between devices, swap(): return lax.ppermute(value, 'ba', [(i, i ^ by) for i in range(n)])  26 us
    ppermute x12, starting transfers between devices, swap(): return lax.ppermute(value, 'ba', [(i, i ^ by) for i in range(n)])  17.5 us
    pallas_call x6, Pallas kernels, kernel(): pl.pallas_call(body, out_shape=outs, in_specs=[VMEM] * (len(given) - hbm)...  12.8 us
    ppermute x1, starting transfers between devices, step(): passed = lax.ppermute(carried, 'aa', pairs)  1.34 us
  transfers between devices with their start and end apart: 13, of which 6 were waited for; matrix products, arithmetic and copies ran while one was open for 2% of the time, Pallas kernels for 19%

profile of v1, /device:TPU:0, one launch (start us, length us, event | category | flops | bytes accessed | tf_op | source)
XLA Modules:
  0.0 62.2 jit_solution(649516205946204748)
XLA Ops:
  0.6 4.1 %collective-permute-start = (bf16[1,64,1024]{2,1,0:T(8,128)(2,1)}, bf16[1,64,1024]{2,1,0:T(8,128)(2,1)S(1)}, u32[]{:S(2)}, u32[]{:S(2)}) collective-permute-start(bf16[1,64,1024]{2,1,0:T(8,128)(2,1)} %param.10), channel_id=1, source_target_pairs={{0,8},{1,9},{2,10},{3,11},{4,12},{5,13},{6,14},{7,15},{8,0},{9,1},... | collective-permute-start | bytes 393224 | tf_op jit(solution)/shard_map/ppermute | solution.py:175
  4.8 6.5 %collective-permute-done = bf16[1,64,1024]{2,1,0:T(8,128)(2,1)S(1)} collective-permute-done((bf16[1,64,1024]{2,1,0:T(8,128)(2,1)}, bf16[1,64,1024]{2,1,0:T(8,128)(2,1)S(1)}, u32[]{:S(2)}, u32[]{:S(2)}) %collective-permute-start) | collective-permute-done | bytes 131104 | tf_op jit(solution)/shard_map/ppermute | solution.py:175
  11.3 0.9 %maximum_bitcast_fusion.near = bf16[2,64,1024]{2,1,0:T(8,128)(2,1)S(1)} fusion(bf16[1,1,64,1024]{3,2,1,0:T(8,128)(2,1)S(1)} %bitcast.33, bf16[1,1,64,1024]{3,2,1,0:T(8,128)(2,1)} %bitcast.32), kind=kLoop, calls=%fused_computation.9 | loop fusion | flops 131072 | bytes 524288 | tf_op jit(solution)/shard_map/reshape | solution.py:207
  12.2 1.6 %collective-permute-start.1 = (bf16[2,64,1024]{2,1,0:T(8,128)(2,1)S(1)}, bf16[2,64,1024]{2,1,0:T(8,128)(2,1)S(1)}, u32[]{:S(2)}, u32[]{:S(2)}) collective-permute-start(bf16[2,64,1024]{2,1,0:T(8,128)(2,1)S(1)} %maximum_bitcast_fusion.near), channel_id=1, source_target_pairs={{0,1},{1,0},{2,3},{3,2},{4,5},{5,4},{6,7},{7,6},{8,9},{9,8},{10,11... | collective-permute-start | bytes 786440 | tf_op jit(solution)/shard_map/ppermute | solution.py:175
  13.8 1.5 %collective-permute-start.5 = (bf16[192,1024]{1,0:T(8,128)(2,1)}, bf16[192,1024]{1,0:T(8,128)(2,1)S(1)}, u32[]{:S(2)}, u32[]{:S(2)}) collective-permute-start(bf16[192,1024]{1,0:T(8,128)(2,1)} %bitcast.16), channel_id=1, source_target_pairs={{0,2},{1,3},{2,0},{3,1},{4,6},{5,7},{6,4},{7,5},{8,10},{9,11},{10,... | collective-permute-start | bytes 1179656 | tf_op jit(solution)/shard_map/ppermute | solution.py:175
  15.3 0.8 %collective-permute-start.2 = (bf16[2,64,1024]{2,1,0:T(8,128)(2,1)S(1)}, bf16[2,64,1024]{2,1,0:T(8,128)(2,1)S(1)}, u32[]{:S(2)}, u32[]{:S(2)}) collective-permute-start(bf16[2,64,1024]{2,1,0:T(8,128)(2,1)S(1)} %maximum_bitcast_fusion.near), channel_id=1, source_target_pairs={{0,4},{1,5},{2,6},{3,7},{4,0},{5,1},{6,2},{7,3},{8,12},{9,13},{10,... | collective-permute-start | bytes 786440 | tf_op jit(solution)/shard_map/ppermute | solution.py:175
  16.1 3.6 %collective-permute-done.1.near_x = bf16[2,64,1024]{2,1,0:T(8,128)(2,1)S(1)} collective-permute-done((bf16[2,64,1024]{2,1,0:T(8,128)(2,1)S(1)}, bf16[2,64,1024]{2,1,0:T(8,128)(2,1)S(1)}, u32[]{:S(2)}, u32[]{:S(2)}) %collective-permute-start.1) | collective-permute-done | bytes 262176 | tf_op jit(solution)/shard_map/ppermute | solution.py:175
  19.7 1.6 %collective-permute-start.3 = (bf16[2,64,1024]{2,1,0:T(8,128)(2,1)S(1)}, bf16[2,64,1024]{2,1,0:T(8,128)(2,1)S(1)}, u32[]{:S(2)}, u32[]{:S(2)}) collective-permute-start(bf16[2,64,1024]{2,1,0:T(8,128)(2,1)S(1)} %collective-permute-done.1.near_x), channel_id=1, source_target_pairs={{0,4},{1,5},{2,6},{3,7},{4,0},{5,1},{6,2},{7,3},{8,12},{9,13},{10,... | collective-permute-start | bytes 786440 | tf_op jit(solution)/shard_map/ppermute | solution.py:175
  21.3 0.7 %copy-done.5 = s32[1,192]{1,0:T(1,128)S(1)} copy-done((s32[1,192]{1,0:T(1,128)S(1)}, s32[1,192]{1,0:T(1,128)}, u32[]{:S(2)}) %copy-start.5) | copy-done | bytes 792
  22.0 4.3 %shard_map.110 = (bf16[192,512]{1,0:T(8,128)(2,1)S(1)}, bf16[192,512]{1,0:T(8,128)(2,1)S(1)}, bf16[16,192,192]{2,1,0:T(8,128)(2,1)}) custom-call(s32[1,192]{1,0:T(1,128)S(1)} %copy-done.5, bf16[192,1024]{1,0:T(8,128)(2,1)} %bitcast.20, bf16[192,1024]{1,0:T(8,128)(2,1)} %bitcast.23, bf16[192,1024]{1,0:T(8,128)(2,1)} %bitcast.26), custom_call_target="tpu_custom_call" | custom-call | flops 603979776 | bytes 1048576 | tf_op jit(solution)/shard_map/pallas_call | solution.py:178
  26.3 0.0 copy-start.1
  26.3 1.6 %collective-permute-start.4 = (bf16[192,512]{1,0:T(8,128)(2,1)S(1)}, bf16[192,512]{1,0:T(8,128)(2,1)S(1)}, u32[]{:S(2)}, u32[]{:S(2)}) collective-permute-start(bf16[192,512]{1,0:T(8,128)(2,1)S(1)} %get-tuple-element.22), channel_id=1, source_target_pairs={{0,2},{1,3},{2,0},{3,1},{4,6},{5,7},{6,4},{7,5},{8,10},{9,11},{10,... | collective-permute-start | bytes 589832 | tf_op jit(solution)/shard_map/ppermute | solution.py:175
  27.9 4.2 %collective-permute-done.4.a_mate = bf16[192,512]{1,0:T(8,128)(2,1)S(1)} collective-permute-done((bf16[192,512]{1,0:T(8,128)(2,1)S(1)}, bf16[192,512]{1,0:T(8,128)(2,1)S(1)}, u32[]{:S(2)}, u32[]{:S(2)}) %collective-permute-start.4) | collective-permute-done | bytes 196640 | tf_op jit(solution)/shard_map/ppermute | solution.py:175
  32.1 0.0 collective-permute-done.2.far
  32.1 0.0 collective-permute-done.5.c_mate
  32.1 0.0 collective-permute-done.3.far_x
  32.1 1.0 %shard_map.111 = (bf16[192,512]{1,0:T(8,128)(2,1)S(1)}, bf16[192,2048]{1,0:T(8,128)(2,1)S(1)}, bf16[512,1024]{1,0:T(8,128)(2,1)S(1)}) custom-call(bf16[2,64,1024]{2,1,0:T(8,128)(2,1)S(1)} %maximum_bitcast_fusion.near, bf16[2,64,1024]{2,1,0:T(8,128)(2,1)S(1)} %collective-permute-done.1.near_x, bf16[2,64,1024]{2,1,0:T(8,128)(2,1)S(1)} %collective-permute-done.2.far, ...), custom_call_target="tpu_custom_call" | custom-call | flops 603979776 | bytes 1048576 | tf_op jit(solution)/shard_map/pallas_call | solution.py:178
  33.1 1.3 %collective-permute-start.6 = (bf16[192,2048]{1,0:T(8,128)(2,1)S(1)}, bf16[192,2048]{1,0:T(8,128)(2,1)S(1)}, u32[]{:S(2)}, u32[]{:S(2)}) collective-permute-start(bf16[192,2048]{1,0:T(8,128)(2,1)S(1)} %get-tuple-element.23), channel_id=1, source_target_pairs={{0,16},{1,17},{2,18},{3,19},{4,20},{5,21},{6,22},{7,23},{8,24},{9,... | collective-permute-start | bytes 2359304 | tf_op jit(solution)/shard_map/ppermute | solution.py:264
  34.5 0.0 copy-done.1
  34.5 0.5 shard_map.115
  35.0 1.5 %collective-permute-start.10 = (bf16[2,64,1024]{2,1,0:T(8,128)(2,1)S(1)}, bf16[2,64,1024]{2,1,0:T(8,128)(2,1)S(1)}, u32[]{:S(2)}, u32[]{:S(2)}) collective-permute-start(bf16[2,64,1024]{2,1,0:T(8,128)(2,1)S(1)} %get-tuple-element.36), channel_id=1, source_target_pairs={{0,1},{1,0},{2,3},{3,2},{4,5},{5,4},{6,7},{7,6},{8,9},{9,8},{10,11... | collective-permute-start | bytes 786440 | tf_op jit(solution)/shard_map/ppermute | solution.py:175
  36.5 0.5 shard_map.114
  37.0 0.6 collective-permute-start.9
  37.6 6.4 %collective-permute-done.10 = bf16[2,64,1024]{2,1,0:T(8,128)(2,1)S(1)} collective-permute-done((bf16[2,64,1024]{2,1,0:T(8,128)(2,1)S(1)}, bf16[2,64,1024]{2,1,0:T(8,128)(2,1)S(1)}, u32[]{:S(2)}, u32[]{:S(2)}) %collective-permute-start.10) | collective-permute-done | bytes 262176 | tf_op jit(solution)/shard_map/ppermute | solution.py:175
  44.0 0.1 add_convert_fusion.1
  44.1 0.2 collective-permute-start.11
  44.3 1.8 %collective-permute-start.8 = (bf16[192,512]{1,0:T(8,128)(2,1)S(1)}, bf16[192,512]{1,0:T(8,128)(2,1)S(1)}, u32[]{:S(2)}, u32[]{:S(2)}) collective-permute-start(bf16[192,512]{1,0:T(8,128)(2,1)S(1)} %get-tuple-element.25), channel_id=1, source_target_pairs={{0,2},{1,3},{2,0},{3,1},{4,6},{5,7},{6,4},{7,5},{8,10},{9,11},{10,... | collective-permute-start | bytes 589832 | tf_op jit(solution)/shard_map/ppermute | solution.py:175
  46.0 0.0 collective-permute-done.6
  46.0 0.3 add_convert_fusion
  46.3 0.0 copy-start
  46.3 0.0 copy-start.2
  46.3 0.0 copy-start.3
  46.4 0.3 collective-permute-start.7
  46.7 0.1 collective-permute-done.9
  46.8 5.1 %collective-permute-done.11 = bf16[2,64,1024]{2,1,0:T(8,128)(2,1)S(1)} collective-permute-done((bf16[2,64,1024]{2,1,0:T(8,128)(2,1)S(1)}, bf16[2,64,1024]{2,1,0:T(8,128)(2,1)S(1)}, u32[]{:S(2)}, u32[]{:S(2)}) %collective-permute-start.11) | collective-permute-done | bytes 262176 | tf_op jit(solution)/shard_map/ppermute | solution.py:175
  51.9 0.1 convert_add_fusion.1
  52.1 1.9 %collective-permute-start.12 = (bf16[1,64,1024]{2,1,0:T(8,128)(2,1)S(1)}, bf16[1,64,1024]{2,1,0:T(8,128)(2,1)S(1)}, u32[]{:S(2)}, u32[]{:S(2)}) collective-permute-start(bf16[1,64,1024]{2,1,0:T(8,128)(2,1)S(1)} %slice.26), channel_id=1, source_target_pairs={{0,8},{1,9},{2,10},{3,11},{4,12},{5,13},{6,14},{7,15},{8,0},{9,1},... | collective-permute-start | bytes 393224 | tf_op jit(solution)/shard_map/ppermute | solution.py:175
  54.0 0.0 copy-done.4
  54.0 0.0 copy-done
  54.0 0.0 copy-done.2
  54.0 3.5 %shard_map.112 = (bf16[192,1024]{1,0:T(8,128)(2,1)}, bf16[192,1024]{1,0:T(8,128)(2,1)}, bf16[192,1024]{1,0:T(8,128)(2,1)}) custom-call(bf16[192,1024]{1,0:T(8,128)(2,1)S(1)} %bitcast.21, bf16[192,1024]{1,0:T(8,128)(2,1)S(1)} %bitcast.24, bf16[192,1024]{1,0:T(8,128)(2,1)S(1)} %bitcast.27, bf16[16,192,192]{2,1,0:T(8,128)(2,1)S(1)} %copy-done, ...), custom_call_target="tpu_custom_call" | custom-call | flops 603979776 | bytes 1048576 | tf_op jit(solution)/shard_map/pallas_call | solution.py:178
  57.5 0.0 collective-permute-done.8.d_ref
  57.5 0.0 copy-start.6
  57.5 3.0 %shard_map.113 = (bf16[192,1024]{1,0:T(8,128)(2,1)}, bf16[192,1024]{1,0:T(8,128)(2,1)}, bf16[192,1024]{1,0:T(8,128)(2,1)}) custom-call(bf16[192,1024]{1,0:T(8,128)(2,1)S(1)} %bitcast.22, bf16[192,1024]{1,0:T(8,128)(2,1)S(1)} %bitcast.25, bf16[192,1024]{1,0:T(8,128)(2,1)S(1)} %bitcast.28, ...), custom_call_target="tpu_custom_call", output_to_operand_aliasing={{0}: (5, {}), {1}: (6, {}), {2}: (7, {})} | custom-call | flops 603979776 | bytes 1048576 | tf_op jit(solution)/shard_map/pallas_call | solution.py:178
  60.5 0.0 collective-permute-done.12
  60.5 0.7 %slice_add_fusion = f32[1,64,1024]{2,1,0:T(8,128)} fusion(f32[2,64,1024]{2,1,0:T(8,128)S(1)} %convert_add_fusion.1, bf16[1,64,1024]{2,1,0:T(8,128)(2,1)S(1)} %collective-permute-done.12), kind=kLoop, calls=%fused_computation.8 | loop fusion | flops 131072 | bytes 655360 | tf_op jit(solution)/shard_map/add | solution.py:252
  61.3 0.0 collective-permute-done.7
  61.3 0.9 %fusion.2 = bf16[1,1,192,1024]{3,2,1,0:T(8,128)(2,1)} fusion(bf16[192,1024]{1,0:T(8,128)(2,1)S(1)} %collective-permute-done.7, bf16[192,2048]{1,0:T(8,128)(2,1)S(1)} %add_convert_fusion, bf16[1,192,1024]{2,1,0:T(8,128)(2,1)S(1)} %copy-done.6), kind=kLoop, calls=%fused_computation.6 | loop fusion | flops 1179648 | bytes 1572864 | tf_op jit(solution)/shard_map/broadcast_in_dim | solution.py:284
  (6 shorter events, 0.1 us)
Async XLA Ops:
  0.6 10.6 %collective-permute-start = (bf16[1,64,1024]{2,1,0:T(8,128)(2,1)}, bf16[1,64,1024]{2,1,0:T(8,128)(2,1)S(1)}, u32[]{:S(2)}, u32[]{:S(2)}) collective-permute-start(bf16[1,64,1024]{2,1,0:T(8,128)(2,1)} %param.10), channel_id=1, source_target_pairs={{0,8},{1,9},{2,10},{3,11},{4,12},{5,13},{6,14},{7,15},{8,0},{9,1},... | collective-permute-start | bytes 393224 | tf_op jit(solution)/shard_map/ppermute | solution.py:175
  12.2 7.5 %collective-permute-start.1 = (bf16[2,64,1024]{2,1,0:T(8,128)(2,1)S(1)}, bf16[2,64,1024]{2,1,0:T(8,128)(2,1)S(1)}, u32[]{:S(2)}, u32[]{:S(2)}) collective-permute-start(bf16[2,64,1024]{2,1,0:T(8,128)(2,1)S(1)} %maximum_bitcast_fusion.near), channel_id=1, source_target_pairs={{0,1},{1,0},{2,3},{3,2},{4,5},{5,4},{6,7},{7,6},{8,9},{9,8},{10,11... | collective-permute-start | bytes 786440 | tf_op jit(solution)/shard_map/ppermute | solution.py:175
  13.8 18.3 %collective-permute-start.5 = (bf16[192,1024]{1,0:T(8,128)(2,1)}, bf16[192,1024]{1,0:T(8,128)(2,1)S(1)}, u32[]{:S(2)}, u32[]{:S(2)}) collective-permute-start(bf16[192,1024]{1,0:T(8,128)(2,1)} %bitcast.16), channel_id=1, source_target_pairs={{0,2},{1,3},{2,0},{3,1},{4,6},{5,7},{6,4},{7,5},{8,10},{9,11},{10,... | collective-permute-start | bytes 1179656 | tf_op jit(solution)/shard_map/ppermute | solution.py:175
  15.3 16.8 %collective-permute-start.2 = (bf16[2,64,1024]{2,1,0:T(8,128)(2,1)S(1)}, bf16[2,64,1024]{2,1,0:T(8,128)(2,1)S(1)}, u32[]{:S(2)}, u32[]{:S(2)}) collective-permute-start(bf16[2,64,1024]{2,1,0:T(8,128)(2,1)S(1)} %maximum_bitcast_fusion.near), channel_id=1, source_target_pairs={{0,4},{1,5},{2,6},{3,7},{4,0},{5,1},{6,2},{7,3},{8,12},{9,13},{10,... | collective-permute-start | bytes 786440 | tf_op jit(solution)/shard_map/ppermute | solution.py:175
  19.7 12.4 %collective-permute-start.3 = (bf16[2,64,1024]{2,1,0:T(8,128)(2,1)S(1)}, bf16[2,64,1024]{2,1,0:T(8,128)(2,1)S(1)}, u32[]{:S(2)}, u32[]{:S(2)}) collective-permute-start(bf16[2,64,1024]{2,1,0:T(8,128)(2,1)S(1)} %collective-permute-done.1.near_x), channel_id=1, source_target_pairs={{0,4},{1,5},{2,6},{3,7},{4,0},{5,1},{6,2},{7,3},{8,12},{9,13},{10,... | collective-permute-start | bytes 786440 | tf_op jit(solution)/shard_map/ppermute | solution.py:175
  21.3 0.7 %copy-start.5 = (s32[1,192]{1,0:T(1,128)S(1)}, s32[1,192]{1,0:T(1,128)}, u32[]{:S(2)}) copy-start(s32[1,192]{1,0:T(1,128)} %ids_hbm.1) | copy-start | bytes 2308
  26.3 8.1 %copy-start.1 = (bf16[1,192,1024]{2,1,0:T(8,128)(2,1)S(1)}, bf16[1,192,1024]{2,1,0:T(8,128)(2,1)}, u32[]{:S(2)}) copy-start(bf16[1,192,1024]{2,1,0:T(8,128)(2,1)} %param.13) | copy-start | bytes 1179652
  26.3 5.7 %collective-permute-start.4 = (bf16[192,512]{1,0:T(8,128)(2,1)S(1)}, bf16[192,512]{1,0:T(8,128)(2,1)S(1)}, u32[]{:S(2)}, u32[]{:S(2)}) collective-permute-start(bf16[192,512]{1,0:T(8,128)(2,1)S(1)} %get-tuple-element.22), channel_id=1, source_target_pairs={{0,2},{1,3},{2,0},{3,1},{4,6},{5,7},{6,4},{7,5},{8,10},{9,11},{10,... | collective-permute-start | bytes 589832 | tf_op jit(solution)/shard_map/ppermute | solution.py:175
  33.1 12.9 %collective-permute-start.6 = (bf16[192,2048]{1,0:T(8,128)(2,1)S(1)}, bf16[192,2048]{1,0:T(8,128)(2,1)S(1)}, u32[]{:S(2)}, u32[]{:S(2)}) collective-permute-start(bf16[192,2048]{1,0:T(8,128)(2,1)S(1)} %get-tuple-element.23), channel_id=1, source_target_pairs={{0,16},{1,17},{2,18},{3,19},{4,20},{5,21},{6,22},{7,23},{8,24},{9,... | collective-permute-start | bytes 2359304 | tf_op jit(solution)/shard_map/ppermute | solution.py:264
  35.0 9.0 %collective-permute-start.10 = (bf16[2,64,1024]{2,1,0:T(8,128)(2,1)S(1)}, bf16[2,64,1024]{2,1,0:T(8,128)(2,1)S(1)}, u32[]{:S(2)}, u32[]{:S(2)}) collective-permute-start(bf16[2,64,1024]{2,1,0:T(8,128)(2,1)S(1)} %get-tuple-element.36), channel_id=1, source_target_pairs={{0,1},{1,0},{2,3},{3,2},{4,5},{5,4},{6,7},{7,6},{8,9},{9,8},{10,11... | collective-permute-start | bytes 786440 | tf_op jit(solution)/shard_map/ppermute | solution.py:175
  37.0 9.8 %collective-permute-start.9 = (bf16[2,64,1024]{2,1,0:T(8,128)(2,1)S(1)}, bf16[2,64,1024]{2,1,0:T(8,128)(2,1)S(1)}, u32[]{:S(2)}, u32[]{:S(2)}) collective-permute-start(bf16[2,64,1024]{2,1,0:T(8,128)(2,1)S(1)} %get-tuple-element.34), channel_id=1, source_target_pairs={{0,1},{1,0},{2,3},{3,2},{4,5},{5,4},{6,7},{7,6},{8,9},{9,8},{10,11... | collective-permute-start | bytes 786440 | tf_op jit(solution)/shard_map/ppermute | solution.py:175
  44.1 7.8 %collective-permute-start.11 = (bf16[2,64,1024]{2,1,0:T(8,128)(2,1)S(1)}, bf16[2,64,1024]{2,1,0:T(8,128)(2,1)S(1)}, u32[]{:S(2)}, u32[]{:S(2)}) collective-permute-start(bf16[2,64,1024]{2,1,0:T(8,128)(2,1)S(1)} %add_convert_fusion.1), channel_id=1, source_target_pairs={{0,4},{1,5},{2,6},{3,7},{4,0},{5,1},{6,2},{7,3},{8,12},{9,13},{10,... | collective-permute-start | bytes 786440 | tf_op jit(solution)/shard_map/ppermute | solution.py:175
  44.3 13.2 %collective-permute-start.8 = (bf16[192,512]{1,0:T(8,128)(2,1)S(1)}, bf16[192,512]{1,0:T(8,128)(2,1)S(1)}, u32[]{:S(2)}, u32[]{:S(2)}) collective-permute-start(bf16[192,512]{1,0:T(8,128)(2,1)S(1)} %get-tuple-element.25), channel_id=1, source_target_pairs={{0,2},{1,3},{2,0},{3,1},{4,6},{5,7},{6,4},{7,5},{8,10},{9,11},{10,... | collective-permute-start | bytes 589832 | tf_op jit(solution)/shard_map/ppermute | solution.py:175
  46.0 8.0 %copy-start.4 = (bf16[1,1,192,1024]{3,2,1,0:T(8,128)(2,1)S(1)}, bf16[1,1,192,1024]{3,2,1,0:T(8,128)(2,1)}, u32[]{:S(2)}) copy-start(bf16[1,1,192,1024]{3,2,1,0:T(8,128)(2,1)} %param.9) | copy-start | bytes 1179652
  46.3 7.7 %copy-start = (bf16[16,192,192]{2,1,0:T(8,128)(2,1)S(1)}, bf16[16,192,192]{2,1,0:T(8,128)(2,1)}, u32[]{:S(2)}) copy-start(bf16[16,192,192]{2,1,0:T(8,128)(2,1)} %get-tuple-element.24.probs) | copy-start | bytes 3538948
  46.3 7.7 %copy-start.2 = (bf16[1,1,192,1024]{3,2,1,0:T(8,128)(2,1)S(1)}, bf16[1,1,192,1024]{3,2,1,0:T(8,128)(2,1)}, u32[]{:S(2)}) copy-start(bf16[1,1,192,1024]{3,2,1,0:T(8,128)(2,1)} %param.7) | copy-start | bytes 1179652
  46.3 7.7 %copy-start.3 = (bf16[1,1,192,1024]{3,2,1,0:T(8,128)(2,1)S(1)}, bf16[1,1,192,1024]{3,2,1,0:T(8,128)(2,1)}, u32[]{:S(2)}) copy-start(bf16[1,1,192,1024]{3,2,1,0:T(8,128)(2,1)} %param.8) | copy-start | bytes 1179652
  46.4 14.9 %collective-permute-start.7 = (bf16[192,1024]{1,0:T(8,128)(2,1)S(1)}, bf16[192,1024]{1,0:T(8,128)(2,1)S(1)}, u32[]{:S(2)}, u32[]{:S(2)}) collective-permute-start(bf16[192,1024]{1,0:T(8,128)(2,1)S(1)} %slice.20), channel_id=1, source_target_pairs={{0,2},{1,3},{2,0},{3,1},{4,6},{5,7},{6,4},{7,5},{8,10},{9,11},{10,... | collective-permute-start | bytes 1179656 | tf_op jit(solution)/shard_map/ppermute | solution.py:175
  52.1 8.5 %collective-permute-start.12 = (bf16[1,64,1024]{2,1,0:T(8,128)(2,1)S(1)}, bf16[1,64,1024]{2,1,0:T(8,128)(2,1)S(1)}, u32[]{:S(2)}, u32[]{:S(2)}) collective-permute-start(bf16[1,64,1024]{2,1,0:T(8,128)(2,1)S(1)} %slice.26), channel_id=1, source_target_pairs={{0,8},{1,9},{2,10},{3,11},{4,12},{5,13},{6,14},{7,15},{8,0},{9,1},... | collective-permute-start | bytes 393224 | tf_op jit(solution)/shard_map/ppermute | solution.py:175
  57.5 3.8 %copy-start.6 = (bf16[1,192,1024]{2,1,0:T(8,128)(2,1)S(1)}, bf16[1,192,1024]{2,1,0:T(8,128)(2,1)}, u32[]{:S(2)}) copy-start(bf16[1,192,1024]{2,1,0:T(8,128)(2,1)} %param.12) | copy-start | bytes 1179652

commit v2 on v1

v2 whole, which is shorter than its diff:
```python
import functools

import jax
import jax.numpy as jnp
from jax import lax
from jax.experimental import pallas as pl
from jax.experimental.pallas import tpu as pltpu
from jax.sharding import PartitionSpec as P


HD = 64
LANES = 128


VMEM = pl.BlockSpec(memory_space=pltpu.VMEM)
HBM = pl.BlockSpec(memory_space=pltpu.HBM)
NT = (((1,), (1,)), ((), ()))
TN = (((0,), (0,)), ((), ()))
IDS_FLOPS = 1 << 32
F32 = jnp.float32
BF16 = jnp.bfloat16


def mul(a, b, dims):
    return lax.dot_general(a, b, dims, preferred_element_type=F32)


def nn(a, b):
    return jnp.dot(a, b, preferred_element_type=F32)


def tile(index):
    return pl.ds(pl.multiple_of(index * LANES, LANES), LANES)


def place_of(bits):
    index = lax.axis_index("ba")
    return (index >> bits) & 1, (index >> (bits - 1)) & 1, index >> (bits + 1)


def in_rows(parts):
    count, share = len(parts), parts[0].shape[0]
    section = lax.axis_index("aa")
    for hop, part in enumerate(parts):
        start = lax.rem(section + count - hop, count) * share
        yield pl.ds(pl.multiple_of(start, share), share), part


def first_head(shape):
    return lax.broadcasted_iota(jnp.int32, shape, 1) < HD


def ids_body(ids, out):
    out[...] = jnp.broadcast_to(ids[...].astype(F32), out.shape)


def forward_body(bits, ids_ref, q_ref, k_ref, v_ref, mine, others, probs):
    own, _, _ = place_of(bits)
    length, inner = q_ref.shape
    pairs = inner // LANES
    ids = ids_ref[...]
    visible = jnp.transpose(ids)[:, :1] <= ids[:1]
    left = first_head((length, LANES))

    def ahead(pair):
        cols = pl.ds(pair * LANES, LANES)
        q_pair = q_ref[:, cols] * (HD**-0.5)
        k_pair = k_ref[:, cols]
        return [mul(jnp.where(left == (half == 0), k_pair, jnp.zeros_like(k_pair)), q_pair, NT) for half in range(2)]

    following = ahead(0)
    for pair in range(pairs):
        scores = following
        if pair + 1 < pairs:
            following = ahead(pair + 1)
        v_pair = v_ref[:, pl.ds(pair * LANES, LANES)]
        halves = []
        for half in range(2):
            seen = jnp.where(visible, scores[half], -jnp.inf)
            lifted = jnp.exp(seen - jnp.max(seen, axis=0, keepdims=True))
            low = (lifted * (1.0 / jnp.sum(lifted, axis=0, keepdims=True))).astype(BF16)
            probs[2 * pair + half] = low
            halves.append(mul(low, v_pair, TN))
        rows = jnp.where(left, halves[0], halves[1]).astype(BF16)
        if pair % 2 == 0:
            even = rows
        else:
            cols = pl.ds((pair // 2) * LANES, LANES)
            mine[:, cols] = jnp.where(own == 0, even, rows)
            others[:, cols] = jnp.where(own == 0, rows, even)


def backward_pairs(refs, probs, jobs, grads, done):
    q_ref, k_ref, v_ref = refs

    def ahead(job):
        pair, d_pair, _ = job
        v_pair = v_ref[:, tile(pair)]
        left = first_head(v_pair.shape)
        return [mul(jnp.where(left == (half == 0), v_pair, jnp.zeros_like(v_pair)), d_pair, NT) for half in range(2)]

    following = ahead(jobs[0])
    for number, (pair, d_pair, block) in enumerate(jobs):
        d_probs = following
        if number + 1 < len(jobs):
            following = ahead(jobs[number + 1])
        cols = tile(pair)
        q_pair = q_ref[:, cols] * (HD**-0.5)
        k_pair = k_ref[:, cols] * (HD**-0.5)
        left = first_head(q_pair.shape)
        got = []
        for half in range(2):
            low = probs[2 * pair + half]
            wide = low.astype(F32)
            delta = jnp.sum(wide * d_probs[half], axis=0, keepdims=True)
            d_scores = (wide * (d_probs[half] - delta)).astype(BF16)
            got.append((mul(d_scores, k_pair, TN), nn(d_scores, q_pair), nn(low, d_pair)))
        for index, (one, two) in enumerate(zip(*got)):
            grads[index, :, block] = jnp.where(left, one, two).astype(BF16)
        done(block, pair)


def backward_own_body(bits, first, q_ref, k_ref, v_ref, probs, c_own, rows, rows_x, *rest):
    own, upper, top = place_of(bits)
    grads = rest[-1] if first else rest[-2]
    jobs = []
    for step in range(rows.shape[0]):
        pair = 2 * (top ^ (2 * step + first)) + own
        block = pl.ds(step * LANES, LANES)
        low = jnp.where(upper == 0, rows[step], rows_x[step])
        high = jnp.where(upper == 0, rows_x[step], rows[step])
        both = jnp.concatenate([low, high], axis=0)
        if first == 0:
            for held, part in in_rows(rest[:-2]):
                rest[-1][held, block] = mul(part[...], both, NT).astype(BF16)
        jobs.append((pair, mul(c_own[...], both, NT).astype(BF16), block))
    backward_pairs((q_ref, k_ref, v_ref), probs, jobs, grads, lambda *_: None)


def backward_mate_body(bits, q_ref, k_ref, v_ref, probs, d_near, d_far, near, far, *rest):
    outs, (grads, sems) = rest[:3], rest[3:]
    own, _, top = place_of(bits)
    tiles = sems.shape[1] // 2
    stores = []

    def store(source, block, pair, slot):
        for index, out in enumerate(outs):
            stores.append(pltpu.make_async_copy(source.at[index, :, block], out.at[:, tile(pair)], sems.at[index, slot]))
            stores[-1].start()

    for distance in range(tiles):
        block = pl.ds(distance // 2 * LANES, LANES)
        store(far if distance % 2 else near, block, 2 * (top ^ distance) + own, distance)
    jobs = []
    for distance in (*range(0, tiles, 2), *range(1, tiles, 2)):
        d_pair = (d_far if distance % 2 else d_near)[:, pl.ds(distance // 2 * LANES, LANES)]
        jobs.append((2 * (top ^ distance) + 1 - own, d_pair, pl.ds(distance * LANES, LANES)))

    def done(block, pair):
        store(grads, block, pair, len(stores) // 3)

    backward_pairs((q_ref, k_ref, v_ref), probs, jobs, grads, done)
    for copy in stores:
        copy.wait()


def finish_body(residual, branches, other, kept, arrived, out, grad_out):
    branch = branches[:, : out.shape[1]].astype(F32)
    out[...] = (residual[...].astype(F32) + branch + other[...].astype(F32)).astype(BF16)
    grad_out[...] = kept[...] + arrived[...].astype(F32)


def product_body(bits, distances, weight, a_own, a_mate, c_own, *rest):
    keep, send = rest[-2:]
    _, upper, top = place_of(bits)
    for step, distance in enumerate(distances):
        cols = tile(jnp.bitwise_xor(top, distance))
        rows = mul(a_own[:, cols], c_own[...], TN)
        for held, part in in_rows(rest[:-2]):
            rows = rows + mul(a_mate[held, cols], part[...], TN)
        rows = rows * weight
        low, high = rows[:HD], rows[HD:]
        keep[step] = jnp.where(upper == 0, low, high)
        send[step] = jnp.where(upper == 0, high, low).astype(BF16)


def weights_body(bits, near, near_x, far, far_x, a_own, a_mate, *rest):
    d_mate, branches, w_out = rest[-3:]
    _, upper, top = place_of(bits)
    half = near.shape[0]
    for distance in range(2 * half):
        mine, other = (far, far_x) if distance % 2 else (near, near_x)
        base = jnp.bitwise_xor(top, distance) * LANES
        step = distance // 2
        w_out[pl.ds(pl.multiple_of(base + upper * HD, HD), HD), :] = mine[step]
        w_out[pl.ds(pl.multiple_of(base + (1 - upper) * HD, HD), HD), :] = other[step]
    res = w_out.shape[1]
    for step in range(half):
        rows = w_out[tile(top ^ (2 * step + 1)), :]
        for held, part in in_rows(rest[:-3]):
            d_mate[held, pl.ds(step * LANES, LANES)] = mul(part[...], rows, NT).astype(BF16)
    branches[:, :res] = nn(a_own[...], w_out[...]).astype(BF16)
    branches[:, res:] = nn(a_mate[...], w_out[...]).astype(BF16)


def step(queries, key_rows, value_rows, out_proj, scale_ids, residual_in, cotangent):
    images, length, inner = queries.shape[1:]
    res = residual_in.shape[2]
    n = lax.axis_size("ba")
    sections = lax.axis_size("aa")
    block = out_proj.shape[1]
    tiles = inner // (2 * LANES)
    bits = (LANES // block).bit_length() - 1
    assert images == 1 and length % sections == 0 and block << bits == LANES and bits > 0 and n == tiles << (bits + 1) and tiles & (tiles - 1) == 0
    weight = 1.0 / (n * images)

    def swap(value, by):
        return lax.ppermute(value, "ba", [(i, i ^ by) for i in range(n)])

    def kernel(body, outs, flops, *given, hbm=0, out_specs=None, aliases={}, scratch=(), limit=24 << 20):
        return pl.pallas_call(
            body,
            out_shape=outs,
            in_specs=[VMEM] * (len(given) - hbm) + [HBM] * hbm,
            out_specs=out_specs or jax.tree.map(lambda _: VMEM, outs),
            input_output_aliases=aliases,
            scratch_shapes=scratch,
            compiler_params=pltpu.CompilerParams(vmem_limit_bytes=limit),
            cost_estimate=pl.CostEstimate(flops=flops, bytes_accessed=1 << 20, transcendentals=0),
        )(*given)

    def shaped(dtype, *dims):
        return jax.ShapeDtypeStruct(dims, dtype)

    index = lax.axis_index("ba")
    mate = 1 << bits
    side = 1 << (bits - 1)
    half = tiles // 2
    levels = tiles.bit_length() - 1
    width = inner // 2

    q, k, v = queries[0, 0], key_rows[0, 0], value_rows[0, 0]
    c_own = cotangent[0]

    section = lax.axis_index("aa")
    share = length // sections
    part = swap(lax.dynamic_slice_in_dim(c_own, section * share, share), mate)
    parts = [part]
    for hop in range(1, sections):
        parts.append(lax.ppermute(part, "aa", [(i, (i + hop) % sections) for i in range(sections)]))
    pairs = [(i, i + 1) for i in range(sections - 1)]
    near = out_proj
    for bit in reversed(range(1, levels)):
        near = jnp.stack([near, swap(near, mate << (bit + 1))], axis=1)
        near = near.reshape(-1, *out_proj.shape[1:])
    for bit in range(bits - 1):
        other = swap(near, 1 << bit)
        odd = ((index >> bit) & 1) == 1
        near = jnp.concatenate([jnp.where(odd, other, near), jnp.where(odd, near, other)], axis=1)
    far = swap(near, mate << 1)
    near_x = swap(near, side)

    far_x = swap(near_x, mate << 1)

    ids = kernel(ids_body, shaped(F32, 8, length), IDS_FLOPS, scale_ids)
    a_own, a_sent, probs = kernel(
        functools.partial(forward_body, bits),
        (shaped(BF16, length, width), shaped(BF16, length, width), shaped(BF16, inner // HD, length, length)),
        16 * length * length * inner,
        ids, q, k, v,
    )
    a_mate = swap(a_sent, mate)

    def product(distances):
        keep, send = kernel(
            functools.partial(product_body, bits, distances, weight),
            (shaped(F32, half, HD, res), shaped(BF16, half, HD, res)),
            4 * length * half * LANES * res,
            a_own, a_mate, c_own, *parts,
        )
        total = keep + swap(send, side).astype(F32)
        for bit in reversed(range(bits - 1)):
            odd = ((index >> bit) & 1) == 1
            low, high = jnp.split(total, 2, axis=1)
            sent = jnp.where(odd, low, high).astype(BF16)
            total = jnp.where(odd, high, low) + swap(sent, 1 << bit).astype(F32)
        return total

    far_sum = product(range(1, tiles, 2))
    near_sum = product(range(0, tiles, 2))
    sums = near_sum + swap(far_sum.astype(BF16), mate << 1).astype(F32)
    for bit in range(1, levels):
        kept, sent = sums[0::2], sums[1::2]
        arrived = swap(sent.astype(BF16), mate << (bit + 1))
        sums = kept + arrived.astype(F32)

    grads_near, d_mate = kernel(
        functools.partial(backward_own_body, bits, 0),
        (shaped(BF16, 3, length, half * LANES), shaped(BF16, length, half * LANES)),
        8 * length * length * inner,
        q, k, v, probs, c_own, near, near_x, *parts,
    )
    d_near = swap(d_mate, mate)

    d_mate, branches = kernel(
        functools.partial(weights_body, bits),
        (shaped(BF16, length, half * LANES), shaped(BF16, length, 2 * res)),
        6 * length * width * res,
        near, near_x, far, far_x, a_own, a_mate, *parts,
        scratch=[pltpu.VMEM((width, res), BF16)],
    )
    d_far = swap(d_mate, mate)
    carried = branches
    for _ in range(sections - 1):
        passed = lax.ppermute(carried, "aa", pairs)
        carried = (branches.astype(F32) + passed.astype(F32)).astype(BF16)
    other = swap(carried[:, res:], mate)
    residual_out, grad_proj = kernel(
        finish_body,
        (shaped(BF16, length, res), shaped(F32, block, res)),
        1 << 20,
        residual_in[0], carried, other, kept[0], arrived[0],
    )

    grads_far = kernel(
        functools.partial(backward_own_body, bits, 1),
        shaped(BF16, 3, length, half * LANES),
        8 * length * length * inner,
        q, k, v, probs, c_own, far, far_x,
    )
    grad_q, grad_k, grad_v = kernel(
        functools.partial(backward_mate_body, bits),
        (shaped(BF16, length, inner),) * 3,
        16 * length * length * inner,
        q, k, v, probs, d_near, d_far, grads_near, grads_far,
        out_specs=(HBM,) * 3,
        scratch=[pltpu.VMEM((3, length, width), BF16), pltpu.SemaphoreType.DMA((3, 2 * tiles))],
    )
    return (
        residual_out[None, None],
        grad_q[None, None],
        grad_k[None, None],
        grad_v[None, None],
        grad_proj[None],
    )


def solution(mesh):
    placed = (
        P("aa", "ba", None, None),
        P("aa", "ba", None, None),
        P("aa", "ba", None, None),
        P("aa", "ba", None),
        P("ba", None),
        P("ba", None, None),
        P("ba", None, None),
    )
    return jax.shard_map(
        step,
        mesh=mesh,
        in_specs=placed,
        out_specs=(
            P("aa", "ba", None, None),
            P("aa", "ba", None, None),
            P("aa", "ba", None, None),
            P("aa", "ba", None, None),
            P("aa", "ba", None),
        ),
        check_vma=False,
    )
```

time: 62.4 us -> 57.4 us (0.920)
  waiting for transfers between devices: 26 us -> 19.2 us
  starting transfers between devices: 18.9 us -> 24.2 us
  Pallas kernels: 12.8 us -> 9.92 us
  other arithmetic: 3 us -> 1.33 us
  local copies, waits for them, and re-layouts: 0.75 us -> 1.71 us
    ppermute x12 -> x13, waiting for transfers between devices: 26 us -> 19.2 us  [swap(): return lax.ppermute(value, 'ba', [(i, i ^ by) for i in range(n)])]
    ppermute x12 -> x13, starting transfers between devices: 17.5 us -> 22.9 us  [swap(): return lax.ppermute(value, 'ba', [(i, i ^ by) for i in range(n)])]
    pallas_call x6 -> x9, Pallas kernels: 12.8 us -> 9.92 us  [kernel(): pl.pallas_call(body, out_shape=outs, in_specs=[VMEM] * (len(given) - hbm)...]
    broadcast_in_dim x1 -> x0, other arithmetic: 0.94 us -> none  [step(): residual_out[None, None]]
    dynamic_slice x0 -> x1, local copies, waits for them, and re-layouts: none -> 0.94 us  [step(): part = swap(lax.dynamic_slice_in_dim(c_own, section * share, share), mate)]
    add x1 -> x0, other arithmetic: 0.73 us -> none  [step(): sums = kept + swap(sent.astype(BF16), mate << bit + 1).astype(F32)]
  transfers between devices with their start and end apart: 13 -> 15, of which waited for: 6 -> 7; matrix products, arithmetic and copies ran while one was open for 2% -> 2% of each run, Pallas kernels for 19% -> 14%
where the time goes in v2:
time: 57.4 us; the launch traced here: 57.2 us
  starting transfers between devices  24.2 us (42%)
  waiting for transfers between devices  19.2 us (33%)
  Pallas kernels  9.92 us (17%)
  local copies, waits for them, and re-layouts  1.71 us (3%)
  other arithmetic  1.33 us (2%)
  between operations  0.83 us (1%)
    ppermute x13, starting transfers between devices, swap(): return lax.ppermute(value, 'ba', [(i, i ^ by) for i in range(n)])  22.9 us
    ppermute x13, waiting for transfers between devices, swap(): return lax.ppermute(value, 'ba', [(i, i ^ by) for i in range(n)])  19.2 us
    pallas_call x9, Pallas kernels, kernel(): pl.pallas_call(body, out_shape=outs, in_specs=[VMEM] * (len(given) - hbm)...  9.92 us
    ppermute x1, starting transfers between devices, step(): passed = lax.ppermute(carried, 'aa', pairs)  1.34 us
  transfers between devices with their start and end apart: 15, of which 7 were waited for; matrix products, arithmetic and copies ran while one was open for 2% of the time, Pallas kernels for 14%

profile of v2, /device:TPU:0, one launch (start us, length us, event | category | flops | bytes accessed | tf_op | source)
XLA Modules:
  0.0 57.2 jit_solution(6496046944793050450)
XLA Ops:
  0.6 4.1 %collective-permute-start = (bf16[1,64,1024]{2,1,0:T(8,128)(2,1)}, bf16[1,64,1024]{2,1,0:T(8,128)(2,1)S(1)}, u32[]{:S(2)}, u32[]{:S(2)}) collective-permute-start(bf16[1,64,1024]{2,1,0:T(8,128)(2,1)} %param.10), channel_id=1, source_target_pairs={{0,8},{1,9},{2,10},{3,11},{4,12},{5,13},{6,14},{7,15},{8,0},{9,1},... | collective-permute-start | bytes 393224 | tf_op jit(solution)/shard_map/ppermute | solution.py:218
  4.8 6.5 %collective-permute-done = bf16[1,64,1024]{2,1,0:T(8,128)(2,1)S(1)} collective-permute-done((bf16[1,64,1024]{2,1,0:T(8,128)(2,1)}, bf16[1,64,1024]{2,1,0:T(8,128)(2,1)S(1)}, u32[]{:S(2)}, u32[]{:S(2)}) %collective-permute-start) | collective-permute-done | bytes 131104 | tf_op jit(solution)/shard_map/ppermute | solution.py:218
  11.3 0.9 %maximum_bitcast_fusion.near.rows = bf16[2,64,1024]{2,1,0:T(8,128)(2,1)S(1)} fusion(bf16[1,1,64,1024]{3,2,1,0:T(8,128)(2,1)S(1)} %bitcast.38, bf16[1,1,64,1024]{3,2,1,0:T(8,128)(2,1)} %bitcast.37), kind=kLoop, calls=%fused_computation.5 | loop fusion | flops 131072 | bytes 524288 | tf_op jit(solution)/shard_map/reshape | solution.py:255
  12.2 1.6 %collective-permute-start.1 = (bf16[2,64,1024]{2,1,0:T(8,128)(2,1)S(1)}, bf16[2,64,1024]{2,1,0:T(8,128)(2,1)S(1)}, u32[]{:S(2)}, u32[]{:S(2)}) collective-permute-start(bf16[2,64,1024]{2,1,0:T(8,128)(2,1)S(1)} %maximum_bitcast_fusion.near.rows), channel_id=1, source_target_pairs={{0,1},{1,0},{2,3},{3,2},{4,5},{5,4},{6,7},{7,6},{8,9},{9,8},{10,11... | collective-permute-start | bytes 786440 | tf_op jit(solution)/shard_map/ppermute | solution.py:218
  13.8 0.9 %dynamic-slice_bitcast_fusion = bf16[96,1024]{1,0:T(8,128)(2,1)S(1)} fusion(bf16[1,192,1024]{2,1,0:T(8,128)(2,1)} %param.13, s32[]{:T(128)S(6)} %select_n.3), kind=kLoop, calls=%fused_computation.6 | loop fusion | bytes 393220 | tf_op jit(solution)/shard_map/dynamic_slice | solution.py:247
  14.8 0.0 copy-start.1
  14.8 0.0 copy-start.2
  14.8 0.0 copy-start.3
  14.8 1.6 %collective-permute-start.5 = (bf16[96,1024]{1,0:T(8,128)(2,1)S(1)}, bf16[96,1024]{1,0:T(8,128)(2,1)S(1)}, u32[]{:S(2)}, u32[]{:S(2)}) collective-permute-start(bf16[96,1024]{1,0:T(8,128)(2,1)S(1)} %dynamic-slice_bitcast_fusion), channel_id=1, source_target_pairs={{0,2},{1,3},{2,0},{3,1},{4,6},{5,7},{6,4},{7,5},{8,10},{9,11},{10,... | collective-permute-start | bytes 589832 | tf_op jit(solution)/shard_map/ppermute | solution.py:218
  16.4 0.8 %collective-permute-start.2 = (bf16[2,64,1024]{2,1,0:T(8,128)(2,1)S(1)}, bf16[2,64,1024]{2,1,0:T(8,128)(2,1)S(1)}, u32[]{:S(2)}, u32[]{:S(2)}) collective-permute-start(bf16[2,64,1024]{2,1,0:T(8,128)(2,1)S(1)} %maximum_bitcast_fusion.near.rows), channel_id=1, source_target_pairs={{0,4},{1,5},{2,6},{3,7},{4,0},{5,1},{6,2},{7,3},{8,12},{9,13},{10,... | collective-permute-start | bytes 786440 | tf_op jit(solution)/shard_map/ppermute | solution.py:218
  17.2 2.6 %collective-permute-done.1.near_x.rows_x = bf16[2,64,1024]{2,1,0:T(8,128)(2,1)S(1)} collective-permute-done((bf16[2,64,1024]{2,1,0:T(8,128)(2,1)S(1)}, bf16[2,64,1024]{2,1,0:T(8,128)(2,1)S(1)}, u32[]{:S(2)}, u32[]{:S(2)}) %collective-permute-start.1) | collective-permute-done | bytes 262176 | tf_op jit(solution)/shard_map/ppermute | solution.py:218
  19.7 1.6 %collective-permute-start.3 = (bf16[2,64,1024]{2,1,0:T(8,128)(2,1)S(1)}, bf16[2,64,1024]{2,1,0:T(8,128)(2,1)S(1)}, u32[]{:S(2)}, u32[]{:S(2)}) collective-permute-start(bf16[2,64,1024]{2,1,0:T(8,128)(2,1)S(1)} %collective-permute-done.1.near_x.rows_x), channel_id=1, source_target_pairs={{0,4},{1,5},{2,6},{3,7},{4,0},{5,1},{6,2},{7,3},{8,12},{9,13},{10,... | collective-permute-start | bytes 786440 | tf_op jit(solution)/shard_map/ppermute | solution.py:218
  21.3 0.7 %copy-done.5 = s32[1,192]{1,0:T(1,128)S(1)} copy-done((s32[1,192]{1,0:T(1,128)S(1)}, s32[1,192]{1,0:T(1,128)}, u32[]{:S(2)}) %copy-start.5) | copy-done | bytes 792
  22.0 2.2 %shard_map.111 = (bf16[192,512]{1,0:T(8,128)(2,1)S(1)}, bf16[192,512]{1,0:T(8,128)(2,1)S(1)}, bf16[16,192,192]{2,1,0:T(8,128)(2,1)S(1)}) custom-call(f32[8,192]{1,0:T(8,128)S(1)} %shard_map.110.ids_ref, bf16[192,1024]{1,0:T(8,128)(2,1)S(1)} %bitcast.23, bf16[192,1024]{1,0:T(8,128)(2,1)S(1)} %bitcast.27, bf16[192,1024]{1,0:T(8,128)(2,1)S(1)} %bitcast.31), custom_call_target="tpu_custom_call" | custom-call | flops 603979776 | bytes 1048576 | tf_op jit(solution)/shard_map/pallas_call | solution.py:221
  24.2 0.0 copy-start
  24.3 1.6 %collective-permute-start.4 = (bf16[192,512]{1,0:T(8,128)(2,1)S(1)}, bf16[192,512]{1,0:T(8,128)(2,1)S(1)}, u32[]{:S(2)}, u32[]{:S(2)}) collective-permute-start(bf16[192,512]{1,0:T(8,128)(2,1)S(1)} %get-tuple-element.22), channel_id=1, source_target_pairs={{0,2},{1,3},{2,0},{3,1},{4,6},{5,7},{6,4},{7,5},{8,10},{9,11},{10,... | collective-permute-start | bytes 589832 | tf_op jit(solution)/shard_map/ppermute | solution.py:218
  25.8 0.0 collective-permute-done.5.rest_0_
  25.8 0.0 collective-permute-start.6
  25.8 4.2 %collective-permute-done.4.a_mate = bf16[192,512]{1,0:T(8,128)(2,1)S(1)} collective-permute-done((bf16[192,512]{1,0:T(8,128)(2,1)S(1)}, bf16[192,512]{1,0:T(8,128)(2,1)S(1)}, u32[]{:S(2)}, u32[]{:S(2)}) %collective-permute-start.4) | collective-permute-done | bytes 196640 | tf_op jit(solution)/shard_map/ppermute | solution.py:218
  30.0 0.0 collective-permute-done.2.far.rows
  30.0 0.0 collective-permute-done.6.rest_1_
  30.0 0.0 collective-permute-done.3.far_x.rows_x
  30.0 1.0 %shard_map.112 = (bf16[192,256]{1,0:T(8,128)(2,1)S(1)}, bf16[192,2048]{1,0:T(8,128)(2,1)S(1)}) custom-call(bf16[2,64,1024]{2,1,0:T(8,128)(2,1)S(1)} %maximum_bitcast_fusion.near.rows, bf16[2,64,1024]{2,1,0:T(8,128)(2,1)S(1)} %collective-permute-done.1.near_x.rows_x, bf16[2,64,1024]{2,1,0:T(8,128)(2,1)S(1)} %collective-permute-done.2.far.rows, ...), custom_call_target="tpu_custom_call" | custom-call | flops 603979776 | bytes 1048576 | tf_op jit(solution)/shard_map/pallas_call | solution.py:221
  31.0 1.3 %collective-permute-start.7 = (bf16[192,2048]{1,0:T(8,128)(2,1)S(1)}, bf16[192,2048]{1,0:T(8,128)(2,1)S(1)}, u32[]{:S(2)}, u32[]{:S(2)}) collective-permute-start(bf16[192,2048]{1,0:T(8,128)(2,1)S(1)} %get-tuple-element.23), channel_id=1, source_target_pairs={{0,16},{1,17},{2,18},{3,19},{4,20},{5,21},{6,22},{7,23},{8,24},{9,... | collective-permute-start | bytes 2359304 | tf_op jit(solution)/shard_map/ppermute | solution.py:315
  32.4 0.6 %shard_map.114 = (f32[2,64,1024]{2,1,0:T(8,128)S(1)}, bf16[2,64,1024]{2,1,0:T(8,128)(2,1)S(1)}) custom-call(bf16[192,512]{1,0:T(8,128)(2,1)S(1)} %get-tuple-element.21.a_own, bf16[192,512]{1,0:T(8,128)(2,1)S(1)} %collective-permute-done.4.a_mate, bf16[192,1024]{1,0:T(8,128)(2,1)S(1)} %bitcast.19, bf16[96,1024]{1,0:T(8,128)(2,1)S(1)} %collective-permute-done.5.rest_0_, ...), custom_call_target="tpu_custom_call" | custom-call | flops 201326592 | bytes 1048576 | tf_op jit(solution)/shard_map/pallas_call | solution.py:221
  33.0 1.6 %collective-permute-start.10 = (bf16[2,64,1024]{2,1,0:T(8,128)(2,1)S(1)}, bf16[2,64,1024]{2,1,0:T(8,128)(2,1)S(1)}, u32[]{:S(2)}, u32[]{:S(2)}) collective-permute-start(bf16[2,64,1024]{2,1,0:T(8,128)(2,1)S(1)} %get-tuple-element.27), channel_id=1, source_target_pairs={{0,1},{1,0},{2,3},{3,2},{4,5},{5,4},{6,7},{7,6},{8,9},{9,8},{10,11... | collective-permute-start | bytes 786440 | tf_op jit(solution)/shard_map/ppermute | solution.py:218
  34.5 1.3 %shard_map.116 = (bf16[3,192,256]{2,1,0:T(8,128)(2,1)S(1)}, bf16[192,256]{1,0:T(8,128)(2,1)S(1)}) custom-call(bf16[192,1024]{1,0:T(8,128)(2,1)S(1)} %bitcast.24, bf16[192,1024]{1,0:T(8,128)(2,1)S(1)} %bitcast.28, bf16[192,1024]{1,0:T(8,128)(2,1)S(1)} %bitcast.32, bf16[16,192,192]{2,1,0:T(8,128)(2,1)S(1)} %get-tuple-element.29.probs, ...), custom_call_target="tpu_custom_call" | custom-call | flops 301989888 | bytes 1048576 | tf_op jit(solution)/shard_map/pallas_call | solution.py:221
  35.9 1.6 %collective-permute-start.13 = (bf16[192,256]{1,0:T(8,128)(2,1)S(1)}, bf16[192,256]{1,0:T(8,128)(2,1)S(1)}, u32[]{:S(2)}, u32[]{:S(2)}) collective-permute-start(bf16[192,256]{1,0:T(8,128)(2,1)S(1)} %get-tuple-element.30), channel_id=1, source_target_pairs={{0,2},{1,3},{2,0},{3,1},{4,6},{5,7},{6,4},{7,5},{8,10},{9,11},{10,... | collective-permute-start | bytes 294920 | tf_op jit(solution)/shard_map/ppermute | solution.py:218
  37.5 0.6 %shard_map.113 = (f32[2,64,1024]{2,1,0:T(8,128)S(1)}, bf16[2,64,1024]{2,1,0:T(8,128)(2,1)S(1)}) custom-call(bf16[192,512]{1,0:T(8,128)(2,1)S(1)} %get-tuple-element.21.a_own, bf16[192,512]{1,0:T(8,128)(2,1)S(1)} %collective-permute-done.4.a_mate, bf16[192,1024]{1,0:T(8,128)(2,1)S(1)} %bitcast.21, bf16[96,1024]{1,0:T(8,128)(2,1)S(1)} %collective-permute-done.5.rest_0_, ...), custom_call_target="tpu_custom_call" | custom-call | flops 201326592 | bytes 1048576 | tf_op jit(solution)/shard_map/pallas_call | solution.py:221
  38.1 0.6 %collective-permute-start.9 = (bf16[2,64,1024]{2,1,0:T(8,128)(2,1)S(1)}, bf16[2,64,1024]{2,1,0:T(8,128)(2,1)S(1)}, u32[]{:S(2)}, u32[]{:S(2)}) collective-permute-start(bf16[2,64,1024]{2,1,0:T(8,128)(2,1)S(1)} %get-tuple-element.25), channel_id=1, source_target_pairs={{0,1},{1,0},{2,3},{3,2},{4,5},{5,4},{6,7},{7,6},{8,9},{9,8},{10,11... | collective-permute-start | bytes 786440 | tf_op jit(solution)/shard_map/ppermute | solution.py:218
  38.7 0.5 collective-permute-start.14
  39.2 1.5 %collective-permute-done.10 = bf16[2,64,1024]{2,1,0:T(8,128)(2,1)S(1)} collective-permute-done((bf16[2,64,1024]{2,1,0:T(8,128)(2,1)S(1)}, bf16[2,64,1024]{2,1,0:T(8,128)(2,1)S(1)}, u32[]{:S(2)}, u32[]{:S(2)}) %collective-permute-start.10) | collective-permute-done | bytes 262176 | tf_op jit(solution)/shard_map/ppermute | solution.py:218
  40.7 0.1 add_convert_fusion.1
  40.7 1.4 %collective-permute-start.11 = (bf16[2,64,1024]{2,1,0:T(8,128)(2,1)S(1)}, bf16[2,64,1024]{2,1,0:T(8,128)(2,1)S(1)}, u32[]{:S(2)}, u32[]{:S(2)}) collective-permute-start(bf16[2,64,1024]{2,1,0:T(8,128)(2,1)S(1)} %add_convert_fusion.1), channel_id=1, source_target_pairs={{0,4},{1,5},{2,6},{3,7},{4,0},{5,1},{6,2},{7,3},{8,12},{9,13},{10,... | collective-permute-start | bytes 786440 | tf_op jit(solution)/shard_map/ppermute | solution.py:218
  42.1 1.1 %shard_map.117.far = bf16[3,192,256]{2,1,0:T(8,128)(2,1)S(1)} custom-call(bf16[192,1024]{1,0:T(8,128)(2,1)S(1)} %bitcast.25, bf16[192,1024]{1,0:T(8,128)(2,1)S(1)} %bitcast.29, bf16[192,1024]{1,0:T(8,128)(2,1)S(1)} %bitcast.33, bf16[16,192,192]{2,1,0:T(8,128)(2,1)S(1)} %get-tuple-element.29.probs, bf16[192,1024]{1,0:T(8,128)(2,1)S(1)} %bitcast.22, ...), custom_call_target="tpu_custom_call" | custom-call | flops 301989888 | bytes 1048576 | tf_op jit(solution)/shard_map/pallas_call | solution.py:221
  43.2 0.0 collective-permute-done.13.d_near
  43.2 0.1 collective-permute-done.14.d_far
  43.3 2.1 %shard_map.118 = (bf16[192,1024]{1,0:T(8,128)(2,1)}, bf16[192,1024]{1,0:T(8,128)(2,1)}, bf16[192,1024]{1,0:T(8,128)(2,1)}) custom-call(bf16[192,1024]{1,0:T(8,128)(2,1)S(1)} %bitcast.26, bf16[192,1024]{1,0:T(8,128)(2,1)S(1)} %bitcast.30, bf16[192,1024]{1,0:T(8,128)(2,1)S(1)} %bitcast.34, bf16[16,192,192]{2,1,0:T(8,128)(2,1)S(1)} %get-tuple-element.29.probs, ...), custom_call_target="tpu_custom_call" | custom-call | flops 603979776 | bytes 1048576 | tf_op jit(solution)/shard_map/pallas_call | solution.py:221
  45.5 0.0 collective-permute-done.7
  45.5 0.3 add_convert_fusion.branches
  45.7 0.0 copy-start.4
  45.8 1.2 %collective-permute-start.8 = (bf16[192,1024]{1,0:T(8,128)(2,1)S(1)}, bf16[192,1024]{1,0:T(8,128)(2,1)S(1)}, u32[]{:S(2)}, u32[]{:S(2)}) collective-permute-start(bf16[192,1024]{1,0:T(8,128)(2,1)S(1)} %slice.15), channel_id=1, source_target_pairs={{0,2},{1,3},{2,0},{3,1},{4,6},{5,7},{6,4},{7,5},{8,10},{9,11},{10,... | collective-permute-start | bytes 1179656 | tf_op jit(solution)/shard_map/ppermute | solution.py:218
  47.0 0.0 collective-permute-done.9
  47.0 0.2 collective-permute-done.11
  47.2 0.1 convert_add_fusion
  47.3 4.7 %collective-permute-start.12 = (bf16[1,64,1024]{2,1,0:T(8,128)(2,1)S(1)}, bf16[1,64,1024]{2,1,0:T(8,128)(2,1)S(1)}, u32[]{:S(2)}, u32[]{:S(2)}) collective-permute-start(bf16[1,64,1024]{2,1,0:T(8,128)(2,1)S(1)} %slice.20), channel_id=1, source_target_pairs={{0,8},{1,9},{2,10},{3,11},{4,12},{5,13},{6,14},{7,15},{8,0},{9,1},... | collective-permute-start | bytes 393224 | tf_op jit(solution)/shard_map/ppermute | solution.py:218
  52.0 4.2 %collective-permute-done.12 = bf16[1,64,1024]{2,1,0:T(8,128)(2,1)S(1)} collective-permute-done((bf16[1,64,1024]{2,1,0:T(8,128)(2,1)S(1)}, bf16[1,64,1024]{2,1,0:T(8,128)(2,1)S(1)}, u32[]{:S(2)}, u32[]{:S(2)}) %collective-permute-start.12) | collective-permute-done | bytes 131104 | tf_op jit(solution)/shard_map/ppermute | solution.py:218
  56.3 1.0 %shard_map.115 = (bf16[192,1024]{1,0:T(8,128)(2,1)}, f32[64,1024]{1,0:T(8,128)}) custom-call(bf16[192,1024]{1,0:T(8,128)(2,1)S(1)} %bitcast.35, bf16[192,2048]{1,0:T(8,128)(2,1)S(1)} %add_convert_fusion.branches, bf16[192,1024]{1,0:T(8,128)(2,1)S(1)} %collective-permute-done.8.other, f32[64,1024]{1,0:T(8,128)S(1)} %slice_bitcast_fusion.kept, ...), custom_call_target="tpu_custom_call" | custom-call | flops 1048576 | bytes 1048576 | tf_op jit(solution)/shard_map/pallas_call | solution.py:221
  (11 shorter events, 0.1 us)
Async XLA Ops:
  0.6 10.6 %collective-permute-start = (bf16[1,64,1024]{2,1,0:T(8,128)(2,1)}, bf16[1,64,1024]{2,1,0:T(8,128)(2,1)S(1)}, u32[]{:S(2)}, u32[]{:S(2)}) collective-permute-start(bf16[1,64,1024]{2,1,0:T(8,128)(2,1)} %param.10), channel_id=1, source_target_pairs={{0,8},{1,9},{2,10},{3,11},{4,12},{5,13},{6,14},{7,15},{8,0},{9,1},... | collective-permute-start | bytes 393224 | tf_op jit(solution)/shard_map/ppermute | solution.py:218
  12.2 7.5 %collective-permute-start.1 = (bf16[2,64,1024]{2,1,0:T(8,128)(2,1)S(1)}, bf16[2,64,1024]{2,1,0:T(8,128)(2,1)S(1)}, u32[]{:S(2)}, u32[]{:S(2)}) collective-permute-start(bf16[2,64,1024]{2,1,0:T(8,128)(2,1)S(1)} %maximum_bitcast_fusion.near.rows), channel_id=1, source_target_pairs={{0,1},{1,0},{2,3},{3,2},{4,5},{5,4},{6,7},{7,6},{8,9},{9,8},{10,11... | collective-permute-start | bytes 786440 | tf_op jit(solution)/shard_map/ppermute | solution.py:218
  14.8 7.3 %copy-start.1 = (bf16[1,1,192,1024]{3,2,1,0:T(8,128)(2,1)S(1)}, bf16[1,1,192,1024]{3,2,1,0:T(8,128)(2,1)}, u32[]{:S(2)}) copy-start(bf16[1,1,192,1024]{3,2,1,0:T(8,128)(2,1)} %param.7) | copy-start | bytes 1179652
  14.8 7.2 %copy-start.2 = (bf16[1,1,192,1024]{3,2,1,0:T(8,128)(2,1)S(1)}, bf16[1,1,192,1024]{3,2,1,0:T(8,128)(2,1)}, u32[]{:S(2)}) copy-start(bf16[1,1,192,1024]{3,2,1,0:T(8,128)(2,1)} %param.8) | copy-start | bytes 1179652
  14.8 7.2 %copy-start.3 = (bf16[1,1,192,1024]{3,2,1,0:T(8,128)(2,1)S(1)}, bf16[1,1,192,1024]{3,2,1,0:T(8,128)(2,1)}, u32[]{:S(2)}) copy-start(bf16[1,1,192,1024]{3,2,1,0:T(8,128)(2,1)} %param.9) | copy-start | bytes 1179652
  14.8 11.0 %collective-permute-start.5 = (bf16[96,1024]{1,0:T(8,128)(2,1)S(1)}, bf16[96,1024]{1,0:T(8,128)(2,1)S(1)}, u32[]{:S(2)}, u32[]{:S(2)}) collective-permute-start(bf16[96,1024]{1,0:T(8,128)(2,1)S(1)} %dynamic-slice_bitcast_fusion), channel_id=1, source_target_pairs={{0,2},{1,3},{2,0},{3,1},{4,6},{5,7},{6,4},{7,5},{8,10},{9,11},{10,... | collective-permute-start | bytes 589832 | tf_op jit(solution)/shard_map/ppermute | solution.py:218
  16.4 13.6 %collective-permute-start.2 = (bf16[2,64,1024]{2,1,0:T(8,128)(2,1)S(1)}, bf16[2,64,1024]{2,1,0:T(8,128)(2,1)S(1)}, u32[]{:S(2)}, u32[]{:S(2)}) collective-permute-start(bf16[2,64,1024]{2,1,0:T(8,128)(2,1)S(1)} %maximum_bitcast_fusion.near.rows), channel_id=1, source_target_pairs={{0,4},{1,5},{2,6},{3,7},{4,0},{5,1},{6,2},{7,3},{8,12},{9,13},{10,... | collective-permute-start | bytes 786440 | tf_op jit(solution)/shard_map/ppermute | solution.py:218
  19.7 10.3 %collective-permute-start.3 = (bf16[2,64,1024]{2,1,0:T(8,128)(2,1)S(1)}, bf16[2,64,1024]{2,1,0:T(8,128)(2,1)S(1)}, u32[]{:S(2)}, u32[]{:S(2)}) collective-permute-start(bf16[2,64,1024]{2,1,0:T(8,128)(2,1)S(1)} %collective-permute-done.1.near_x.rows_x), channel_id=1, source_target_pairs={{0,4},{1,5},{2,6},{3,7},{4,0},{5,1},{6,2},{7,3},{8,12},{9,13},{10,... | collective-permute-start | bytes 786440 | tf_op jit(solution)/shard_map/ppermute | solution.py:218
  21.3 0.7 %copy-start.5 = (s32[1,192]{1,0:T(1,128)S(1)}, s32[1,192]{1,0:T(1,128)}, u32[]{:S(2)}) copy-start(s32[1,192]{1,0:T(1,128)} %ids.1) | copy-start | bytes 2308
  24.2 8.1 %copy-start = (bf16[1,192,1024]{2,1,0:T(8,128)(2,1)S(1)}, bf16[1,192,1024]{2,1,0:T(8,128)(2,1)}, u32[]{:S(2)}) copy-start(bf16[1,192,1024]{2,1,0:T(8,128)(2,1)} %param.13) | copy-start | bytes 1179652
  24.3 5.7 %collective-permute-start.4 = (bf16[192,512]{1,0:T(8,128)(2,1)S(1)}, bf16[192,512]{1,0:T(8,128)(2,1)S(1)}, u32[]{:S(2)}, u32[]{:S(2)}) collective-permute-start(bf16[192,512]{1,0:T(8,128)(2,1)S(1)} %get-tuple-element.22), channel_id=1, source_target_pairs={{0,2},{1,3},{2,0},{3,1},{4,6},{5,7},{6,4},{7,5},{8,10},{9,11},{10,... | collective-permute-start | bytes 589832 | tf_op jit(solution)/shard_map/ppermute | solution.py:218
  25.8 4.2 %collective-permute-start.6 = (bf16[96,1024]{1,0:T(8,128)(2,1)S(1)}, bf16[96,1024]{1,0:T(8,128)(2,1)S(1)}, u32[]{:S(2)}, u32[]{:S(2)}) collective-permute-start(bf16[96,1024]{1,0:T(8,128)(2,1)S(1)} %collective-permute-done.5.rest_0_), channel_id=1, source_target_pairs={{0,16},{16,0},{1,17},{17,1},{2,18},{18,2},{3,19},{19,3},{4,20},{20... | collective-permute-start | bytes 589832 | tf_op jit(solution)/shard_map/ppermute | solution.py:250
  31.0 14.5 %collective-permute-start.7 = (bf16[192,2048]{1,0:T(8,128)(2,1)S(1)}, bf16[192,2048]{1,0:T(8,128)(2,1)S(1)}, u32[]{:S(2)}, u32[]{:S(2)}) collective-permute-start(bf16[192,2048]{1,0:T(8,128)(2,1)S(1)} %get-tuple-element.23), channel_id=1, source_target_pairs={{0,16},{1,17},{2,18},{3,19},{4,20},{5,21},{6,22},{7,23},{8,24},{9,... | collective-permute-start | bytes 2359304 | tf_op jit(solution)/shard_map/ppermute | solution.py:315
  33.0 7.7 %collective-permute-start.10 = (bf16[2,64,1024]{2,1,0:T(8,128)(2,1)S(1)}, bf16[2,64,1024]{2,1,0:T(8,128)(2,1)S(1)}, u32[]{:S(2)}, u32[]{:S(2)}) collective-permute-start(bf16[2,64,1024]{2,1,0:T(8,128)(2,1)S(1)} %get-tuple-element.27), channel_id=1, source_target_pairs={{0,1},{1,0},{2,3},{3,2},{4,5},{5,4},{6,7},{7,6},{8,9},{9,8},{10,11... | collective-permute-start | bytes 786440 | tf_op jit(solution)/shard_map/ppermute | solution.py:218
  35.9 7.3 %collective-permute-start.13 = (bf16[192,256]{1,0:T(8,128)(2,1)S(1)}, bf16[192,256]{1,0:T(8,128)(2,1)S(1)}, u32[]{:S(2)}, u32[]{:S(2)}) collective-permute-start(bf16[192,256]{1,0:T(8,128)(2,1)S(1)} %get-tuple-element.30), channel_id=1, source_target_pairs={{0,2},{1,3},{2,0},{3,1},{4,6},{5,7},{6,4},{7,5},{8,10},{9,11},{10,... | collective-permute-start | bytes 294920 | tf_op jit(solution)/shard_map/ppermute | solution.py:218
  38.1 8.9 %collective-permute-start.9 = (bf16[2,64,1024]{2,1,0:T(8,128)(2,1)S(1)}, bf16[2,64,1024]{2,1,0:T(8,128)(2,1)S(1)}, u32[]{:S(2)}, u32[]{:S(2)}) collective-permute-start(bf16[2,64,1024]{2,1,0:T(8,128)(2,1)S(1)} %get-tuple-element.25), channel_id=1, source_target_pairs={{0,1},{1,0},{2,3},{3,2},{4,5},{5,4},{6,7},{7,6},{8,9},{9,8},{10,11... | collective-permute-start | bytes 786440 | tf_op jit(solution)/shard_map/ppermute | solution.py:218
  38.7 4.6 %collective-permute-start.14 = (bf16[192,256]{1,0:T(8,128)(2,1)S(1)}, bf16[192,256]{1,0:T(8,128)(2,1)S(1)}, u32[]{:S(2)}, u32[]{:S(2)}) collective-permute-start(bf16[192,256]{1,0:T(8,128)(2,1)S(1)} %get-tuple-element.31), channel_id=1, source_target_pairs={{0,2},{1,3},{2,0},{3,1},{4,6},{5,7},{6,4},{7,5},{8,10},{9,11},{10,... | collective-permute-start | bytes 294920 | tf_op jit(solution)/shard_map/ppermute | solution.py:218
  40.7 6.4 %collective-permute-start.11 = (bf16[2,64,1024]{2,1,0:T(8,128)(2,1)S(1)}, bf16[2,64,1024]{2,1,0:T(8,128)(2,1)S(1)}, u32[]{:S(2)}, u32[]{:S(2)}) collective-permute-start(bf16[2,64,1024]{2,1,0:T(8,128)(2,1)S(1)} %add_convert_fusion.1), channel_id=1, source_target_pairs={{0,4},{1,5},{2,6},{3,7},{4,0},{5,1},{6,2},{7,3},{8,12},{9,13},{10,... | collective-permute-start | bytes 786440 | tf_op jit(solution)/shard_map/ppermute | solution.py:218
  45.7 10.5 %copy-start.4 = (bf16[1,192,1024]{2,1,0:T(8,128)(2,1)S(1)}, bf16[1,192,1024]{2,1,0:T(8,128)(2,1)}, u32[]{:S(2)}) copy-start(bf16[1,192,1024]{2,1,0:T(8,128)(2,1)} %param.12) | copy-start | bytes 1179652
  45.8 10.5 %collective-permute-start.8 = (bf16[192,1024]{1,0:T(8,128)(2,1)S(1)}, bf16[192,1024]{1,0:T(8,128)(2,1)S(1)}, u32[]{:S(2)}, u32[]{:S(2)}) collective-permute-start(bf16[192,1024]{1,0:T(8,128)(2,1)S(1)} %slice.15), channel_id=1, source_target_pairs={{0,2},{1,3},{2,0},{3,1},{4,6},{5,7},{6,4},{7,5},{8,10},{9,11},{10,... | collective-permute-start | bytes 1179656 | tf_op jit(solution)/shard_map/ppermute | solution.py:218
  47.3 9.0 %collective-permute-start.12 = (bf16[1,64,1024]{2,1,0:T(8,128)(2,1)S(1)}, bf16[1,64,1024]{2,1,0:T(8,128)(2,1)S(1)}, u32[]{:S(2)}, u32[]{:S(2)}) collective-permute-start(bf16[1,64,1024]{2,1,0:T(8,128)(2,1)S(1)} %slice.20), channel_id=1, source_target_pairs={{0,8},{1,9},{2,10},{3,11},{4,12},{5,13},{6,14},{7,15},{8,0},{9,1},... | collective-permute-start | bytes 393224 | tf_op jit(solution)/shard_map/ppermute | solution.py:218

commit v3 on v2

--- a/solution.py
+++ b/solution.py
@@ -16,7 +16,7 @@
 HBM = pl.BlockSpec(memory_space=pltpu.HBM)
 NT = (((1,), (1,)), ((), ()))
 TN = (((0,), (0,)), ((), ()))
-IDS_FLOPS = 1 << 32
+FIRST_FLOPS = 1 << 32
 F32 = jnp.float32
 BF16 = jnp.bfloat16
 
@@ -50,17 +50,17 @@
     return lax.broadcasted_iota(jnp.int32, shape, 1) < HD
 
 
-def ids_body(ids, out):
-    out[...] = jnp.broadcast_to(ids[...].astype(F32), out.shape)
-
-
-def forward_body(bits, ids_ref, q_ref, k_ref, v_ref, mine, others, probs):
+def first_body(out):
+    out[...] = first_head(out.shape).astype(F32)
+
+
+def forward_body(bits, lanes, ids_ref, q_ref, k_ref, v_ref, mine, others, probs):
     own, _, _ = place_of(bits)
     length, inner = q_ref.shape
     pairs = inner // LANES
-    ids = ids_ref[...]
+    ids = jnp.broadcast_to(ids_ref[...].astype(F32), (lanes.shape[0], length))
     visible = jnp.transpose(ids)[:, :1] <= ids[:1]
-    left = first_head((length, LANES))
+    left = jnp.broadcast_to(lanes[:1], (length, LANES)) > 0.5
 
     def ahead(pair):
         cols = pl.ds(pair * LANES, LANES)
@@ -164,10 +164,20 @@
         copy.wait()
 
 
-def finish_body(residual, branches, other, kept, arrived, out, grad_out):
-    branch = branches[:, : out.shape[1]].astype(F32)
-    out[...] = (residual[...].astype(F32) + branch + other[...].astype(F32)).astype(BF16)
-    grad_out[...] = kept[...] + arrived[...].astype(F32)
+def finish_body(residual, branches, other, kept, arrived, out, grad_out, total, grad_total, sems):
+    length, res = total.shape
+    grad_total[...] = kept[...] + arrived[...].astype(F32)
+    copies = [pltpu.make_async_copy(grad_total, grad_out, sems.at[0])]
+    copies[0].start()
+    share = length // (sems.shape[0] - 1)
+    for part in range(sems.shape[0] - 1):
+        rows = pl.ds(part * share, share)
+        branch = branches[rows, :res].astype(F32) + other[rows].astype(F32)
+        total[rows] = (residual[rows].astype(F32) + branch).astype(BF16)
+        copies.append(pltpu.make_async_copy(total.at[rows], out.at[rows], sems.at[part + 1]))
+        copies[-1].start()
+    for copy in copies:
+        copy.wait()
 
 
 def product_body(bits, distances, weight, a_own, a_mate, c_own, *rest):
@@ -262,12 +272,12 @@
 
     far_x = swap(near_x, mate << 1)
 
-    ids = kernel(ids_body, shaped(F32, 8, length), IDS_FLOPS, scale_ids)
+    lanes = kernel(first_body, shaped(F32, 8, LANES), FIRST_FLOPS)
     a_own, a_sent, probs = kernel(
         functools.partial(forward_body, bits),
         (shaped(BF16, length, width), shaped(BF16, length, width), shaped(BF16, inner // HD, length, length)),
         16 * length * length * inner,
-        ids, q, k, v,
+        lanes, scale_ids, q, k, v,
     )
     a_mate = swap(a_sent, mate)
 
@@ -320,6 +330,8 @@
         (shaped(BF16, length, res), shaped(F32, block, res)),
         1 << 20,
         residual_in[0], carried, other, kept[0], arrived[0],
+        out_specs=(HBM, HBM),
+        scratch=[pltpu.VMEM((length, res), BF16), pltpu.VMEM((block, res), F32), pltpu.SemaphoreType.DMA((4,))],
     )
 
     grads_far = kernel(

time: 57.4 us -> 57.2 us (level)
  waiting for transfers between devices: 19.2 us -> 20.6 us
  starting transfers between devices: 24.2 us -> 23.3 us
  local copies, waits for them, and re-layouts: 1.71 us -> 1.04 us
    ppermute x13, waiting for transfers between devices: 19.2 us -> 20.6 us  [swap(): return lax.ppermute(value, 'ba', [(i, i ^ by) for i in range(n)])]
    ppermute x13, starting transfers between devices: 22.9 us -> 22 us  [swap(): return lax.ppermute(value, 'ba', [(i, i ^ by) for i in range(n)])]
    unnamed x12, local copies, waits for them, and re-layouts: 0.71 us -> 0.04 us
  transfers between devices with their start and end apart: 15 -> 15, of which waited for: 7 -> 6; matrix products, arithmetic and copies ran while one was open for 2% -> 2% of each run, Pallas kernels for 14% -> 14%
where the time goes in v3:
time: 57.2 us; the launch traced here: 57 us
  starting transfers between devices  23.3 us (41%)
  waiting for transfers between devices  20.6 us (36%)
  Pallas kernels  9.87 us (17%)
  other arithmetic  1.33 us (2%)
  local copies, waits for them, and re-layouts  1.04 us (2%)
  between operations  0.85 us (1%)
    ppermute x13, starting transfers between devices, swap(): return lax.ppermute(value, 'ba', [(i, i ^ by) for i in range(n)])  22 us
    ppermute x13, waiting for transfers between devices, swap(): return lax.ppermute(value, 'ba', [(i, i ^ by) for i in range(n)])  20.6 us
    pallas_call x9, Pallas kernels, kernel(): pl.pallas_call(body, out_shape=outs, in_specs=[VMEM] * (len(given) - hbm)...  9.87 us
    ppermute x1, starting transfers between devices, step(): passed = lax.ppermute(carried, 'aa', pairs)  1.34 us
  transfers between devices with their start and end apart: 15, of which 6 were waited for; matrix products, arithmetic and copies ran while one was open for 2% of the time, Pallas kernels for 14%

profile of v3, /device:TPU:0, one launch (start us, length us, event | category | flops | bytes accessed | tf_op | source)
XLA Modules:
  0.0 57.0 jit_solution(7564713902114483167)
XLA Ops:
  0.6 4.1 %collective-permute-start = (bf16[1,64,1024]{2,1,0:T(8,128)(2,1)}, bf16[1,64,1024]{2,1,0:T(8,128)(2,1)S(1)}, u32[]{:S(2)}, u32[]{:S(2)}) collective-permute-start(bf16[1,64,1024]{2,1,0:T(8,128)(2,1)} %param.10), channel_id=1, source_target_pairs={{0,8},{1,9},{2,10},{3,11},{4,12},{5,13},{6,14},{7,15},{8,0},{9,1},... | collective-permute-start | bytes 393224 | tf_op jit(solution)/shard_map/ppermute | solution.py:228
  4.8 6.5 %collective-permute-done = bf16[1,64,1024]{2,1,0:T(8,128)(2,1)S(1)} collective-permute-done((bf16[1,64,1024]{2,1,0:T(8,128)(2,1)}, bf16[1,64,1024]{2,1,0:T(8,128)(2,1)S(1)}, u32[]{:S(2)}, u32[]{:S(2)}) %collective-permute-start) | collective-permute-done | bytes 131104 | tf_op jit(solution)/shard_map/ppermute | solution.py:228
  11.3 0.9 %maximum_bitcast_fusion.near.rows = bf16[2,64,1024]{2,1,0:T(8,128)(2,1)S(1)} fusion(bf16[1,1,64,1024]{3,2,1,0:T(8,128)(2,1)S(1)} %bitcast.38, bf16[1,1,64,1024]{3,2,1,0:T(8,128)(2,1)} %bitcast.37), kind=kLoop, calls=%fused_computation.5 | loop fusion | flops 131072 | bytes 524288 | tf_op jit(solution)/shard_map/reshape | solution.py:265
  12.2 1.6 %collective-permute-start.1 = (bf16[2,64,1024]{2,1,0:T(8,128)(2,1)S(1)}, bf16[2,64,1024]{2,1,0:T(8,128)(2,1)S(1)}, u32[]{:S(2)}, u32[]{:S(2)}) collective-permute-start(bf16[2,64,1024]{2,1,0:T(8,128)(2,1)S(1)} %maximum_bitcast_fusion.near.rows), channel_id=1, source_target_pairs={{0,1},{1,0},{2,3},{3,2},{4,5},{5,4},{6,7},{7,6},{8,9},{9,8},{10,11... | collective-permute-start | bytes 786440 | tf_op jit(solution)/shard_map/ppermute | solution.py:228
  13.8 0.9 %dynamic-slice_bitcast_fusion = bf16[96,1024]{1,0:T(8,128)(2,1)S(1)} fusion(bf16[1,192,1024]{2,1,0:T(8,128)(2,1)} %param.13, s32[]{:T(128)S(6)} %select_n.3), kind=kLoop, calls=%fused_computation.6 | loop fusion | bytes 393220 | tf_op jit(solution)/shard_map/dynamic_slice | solution.py:257
  14.8 0.0 copy-start.1
  14.8 0.0 copy-start.2
  14.8 0.0 copy-start.3
  14.8 0.0 copy-start.5
  14.8 1.6 %collective-permute-start.5 = (bf16[96,1024]{1,0:T(8,128)(2,1)S(1)}, bf16[96,1024]{1,0:T(8,128)(2,1)S(1)}, u32[]{:S(2)}, u32[]{:S(2)}) collective-permute-start(bf16[96,1024]{1,0:T(8,128)(2,1)S(1)} %dynamic-slice_bitcast_fusion), channel_id=1, source_target_pairs={{0,2},{1,3},{2,0},{3,1},{4,6},{5,7},{6,4},{7,5},{8,10},{9,11},{10,... | collective-permute-start | bytes 589832 | tf_op jit(solution)/shard_map/ppermute | solution.py:228
  16.4 0.8 %collective-permute-start.2 = (bf16[2,64,1024]{2,1,0:T(8,128)(2,1)S(1)}, bf16[2,64,1024]{2,1,0:T(8,128)(2,1)S(1)}, u32[]{:S(2)}, u32[]{:S(2)}) collective-permute-start(bf16[2,64,1024]{2,1,0:T(8,128)(2,1)S(1)} %maximum_bitcast_fusion.near.rows), channel_id=1, source_target_pairs={{0,4},{1,5},{2,6},{3,7},{4,0},{5,1},{6,2},{7,3},{8,12},{9,13},{10,... | collective-permute-start | bytes 786440 | tf_op jit(solution)/shard_map/ppermute | solution.py:228
  17.2 2.6 %collective-permute-done.1.near_x.rows_x = bf16[2,64,1024]{2,1,0:T(8,128)(2,1)S(1)} collective-permute-done((bf16[2,64,1024]{2,1,0:T(8,128)(2,1)S(1)}, bf16[2,64,1024]{2,1,0:T(8,128)(2,1)S(1)}, u32[]{:S(2)}, u32[]{:S(2)}) %collective-permute-start.1) | collective-permute-done | bytes 262176 | tf_op jit(solution)/shard_map/ppermute | solution.py:228
  19.7 1.6 %collective-permute-start.3 = (bf16[2,64,1024]{2,1,0:T(8,128)(2,1)S(1)}, bf16[2,64,1024]{2,1,0:T(8,128)(2,1)S(1)}, u32[]{:S(2)}, u32[]{:S(2)}) collective-permute-start(bf16[2,64,1024]{2,1,0:T(8,128)(2,1)S(1)} %collective-permute-done.1.near_x.rows_x), channel_id=1, source_target_pairs={{0,4},{1,5},{2,6},{3,7},{4,0},{5,1},{6,2},{7,3},{8,12},{9,13},{10,... | collective-permute-start | bytes 786440 | tf_op jit(solution)/shard_map/ppermute | solution.py:228
  21.4 2.2 %shard_map.111 = (bf16[192,512]{1,0:T(8,128)(2,1)S(1)}, bf16[192,512]{1,0:T(8,128)(2,1)S(1)}, bf16[16,192,192]{2,1,0:T(8,128)(2,1)S(1)}) custom-call(f32[8,128]{1,0:T(8,128)S(1)} %shard_map.110.lanes, s32[1,192]{1,0:T(1,128)S(1)} %copy-done.5, bf16[192,1024]{1,0:T(8,128)(2,1)S(1)} %bitcast.23, bf16[192,1024]{1,0:T(8,128)(2,1)S(1)} %bitcast.27, ...), custom_call_target="tpu_custom_call" | custom-call | flops 603979776 | bytes 1048576 | tf_op jit(solution)/shard_map/pallas_call | solution.py:231
  23.6 0.0 copy-start
  23.6 1.6 %collective-permute-start.4 = (bf16[192,512]{1,0:T(8,128)(2,1)S(1)}, bf16[192,512]{1,0:T(8,128)(2,1)S(1)}, u32[]{:S(2)}, u32[]{:S(2)}) collective-permute-start(bf16[192,512]{1,0:T(8,128)(2,1)S(1)} %get-tuple-element.22), channel_id=1, source_target_pairs={{0,2},{1,3},{2,0},{3,1},{4,6},{5,7},{6,4},{7,5},{8,10},{9,11},{10,... | collective-permute-start | bytes 589832 | tf_op jit(solution)/shard_map/ppermute | solution.py:228
  25.2 0.0 collective-permute-done.5.rest_0_
  25.2 0.0 collective-permute-start.6
  25.2 4.2 %collective-permute-done.4.a_mate = bf16[192,512]{1,0:T(8,128)(2,1)S(1)} collective-permute-done((bf16[192,512]{1,0:T(8,128)(2,1)S(1)}, bf16[192,512]{1,0:T(8,128)(2,1)S(1)}, u32[]{:S(2)}, u32[]{:S(2)}) %collective-permute-start.4) | collective-permute-done | bytes 196640 | tf_op jit(solution)/shard_map/ppermute | solution.py:228
  29.3 0.0 collective-permute-done.2.far.rows
  29.4 0.0 collective-permute-done.6.rest_1_
  29.4 0.0 collective-permute-done.3.far_x.rows_x
  29.4 1.0 %shard_map.112 = (bf16[192,256]{1,0:T(8,128)(2,1)S(1)}, bf16[192,2048]{1,0:T(8,128)(2,1)S(1)}) custom-call(bf16[2,64,1024]{2,1,0:T(8,128)(2,1)S(1)} %maximum_bitcast_fusion.near.rows, bf16[2,64,1024]{2,1,0:T(8,128)(2,1)S(1)} %collective-permute-done.1.near_x.rows_x, bf16[2,64,1024]{2,1,0:T(8,128)(2,1)S(1)} %collective-permute-done.2.far.rows, ...), custom_call_target="tpu_custom_call" | custom-call | flops 603979776 | bytes 1048576 | tf_op jit(solution)/shard_map/pallas_call | solution.py:231
  30.3 1.3 %collective-permute-start.7 = (bf16[192,2048]{1,0:T(8,128)(2,1)S(1)}, bf16[192,2048]{1,0:T(8,128)(2,1)S(1)}, u32[]{:S(2)}, u32[]{:S(2)}) collective-permute-start(bf16[192,2048]{1,0:T(8,128)(2,1)S(1)} %get-tuple-element.23), channel_id=1, source_target_pairs={{0,16},{1,17},{2,18},{3,19},{4,20},{5,21},{6,22},{7,23},{8,24},{9,... | collective-permute-start | bytes 2359304 | tf_op jit(solution)/shard_map/ppermute | solution.py:325
  31.7 0.6 %shard_map.114 = (f32[2,64,1024]{2,1,0:T(8,128)S(1)}, bf16[2,64,1024]{2,1,0:T(8,128)(2,1)S(1)}) custom-call(bf16[192,512]{1,0:T(8,128)(2,1)S(1)} %get-tuple-element.21.a_own, bf16[192,512]{1,0:T(8,128)(2,1)S(1)} %collective-permute-done.4.a_mate, bf16[192,1024]{1,0:T(8,128)(2,1)S(1)} %bitcast.19, bf16[96,1024]{1,0:T(8,128)(2,1)S(1)} %collective-permute-done.5.rest_0_, ...), custom_call_target="tpu_custom_call" | custom-call | flops 201326592 | bytes 1048576 | tf_op jit(solution)/shard_map/pallas_call | solution.py:231
  32.3 1.6 %collective-permute-start.10 = (bf16[2,64,1024]{2,1,0:T(8,128)(2,1)S(1)}, bf16[2,64,1024]{2,1,0:T(8,128)(2,1)S(1)}, u32[]{:S(2)}, u32[]{:S(2)}) collective-permute-start(bf16[2,64,1024]{2,1,0:T(8,128)(2,1)S(1)} %get-tuple-element.27), channel_id=1, source_target_pairs={{0,1},{1,0},{2,3},{3,2},{4,5},{5,4},{6,7},{7,6},{8,9},{9,8},{10,11... | collective-permute-start | bytes 786440 | tf_op jit(solution)/shard_map/ppermute | solution.py:228
  33.9 1.3 %shard_map.116 = (bf16[3,192,256]{2,1,0:T(8,128)(2,1)S(1)}, bf16[192,256]{1,0:T(8,128)(2,1)S(1)}) custom-call(bf16[192,1024]{1,0:T(8,128)(2,1)S(1)} %bitcast.24, bf16[192,1024]{1,0:T(8,128)(2,1)S(1)} %bitcast.28, bf16[192,1024]{1,0:T(8,128)(2,1)S(1)} %bitcast.32, bf16[16,192,192]{2,1,0:T(8,128)(2,1)S(1)} %get-tuple-element.29.probs, ...), custom_call_target="tpu_custom_call" | custom-call | flops 301989888 | bytes 1048576 | tf_op jit(solution)/shard_map/pallas_call | solution.py:231
  35.2 1.6 %collective-permute-start.13 = (bf16[192,256]{1,0:T(8,128)(2,1)S(1)}, bf16[192,256]{1,0:T(8,128)(2,1)S(1)}, u32[]{:S(2)}, u32[]{:S(2)}) collective-permute-start(bf16[192,256]{1,0:T(8,128)(2,1)S(1)} %get-tuple-element.30), channel_id=1, source_target_pairs={{0,2},{1,3},{2,0},{3,1},{4,6},{5,7},{6,4},{7,5},{8,10},{9,11},{10,... | collective-permute-start | bytes 294920 | tf_op jit(solution)/shard_map/ppermute | solution.py:228
  36.8 0.6 %shard_map.113 = (f32[2,64,1024]{2,1,0:T(8,128)S(1)}, bf16[2,64,1024]{2,1,0:T(8,128)(2,1)S(1)}) custom-call(bf16[192,512]{1,0:T(8,128)(2,1)S(1)} %get-tuple-element.21.a_own, bf16[192,512]{1,0:T(8,128)(2,1)S(1)} %collective-permute-done.4.a_mate, bf16[192,1024]{1,0:T(8,128)(2,1)S(1)} %bitcast.21, bf16[96,1024]{1,0:T(8,128)(2,1)S(1)} %collective-permute-done.5.rest_0_, ...), custom_call_target="tpu_custom_call" | custom-call | flops 201326592 | bytes 1048576 | tf_op jit(solution)/shard_map/pallas_call | solution.py:231
  37.4 0.6 %collective-permute-start.9 = (bf16[2,64,1024]{2,1,0:T(8,128)(2,1)S(1)}, bf16[2,64,1024]{2,1,0:T(8,128)(2,1)S(1)}, u32[]{:S(2)}, u32[]{:S(2)}) collective-permute-start(bf16[2,64,1024]{2,1,0:T(8,128)(2,1)S(1)} %get-tuple-element.25), channel_id=1, source_target_pairs={{0,1},{1,0},{2,3},{3,2},{4,5},{5,4},{6,7},{7,6},{8,9},{9,8},{10,11... | collective-permute-start | bytes 786440 | tf_op jit(solution)/shard_map/ppermute | solution.py:228
  38.1 0.5 collective-permute-start.14
  38.6 1.5 %collective-permute-done.10 = bf16[2,64,1024]{2,1,0:T(8,128)(2,1)S(1)} collective-permute-done((bf16[2,64,1024]{2,1,0:T(8,128)(2,1)S(1)}, bf16[2,64,1024]{2,1,0:T(8,128)(2,1)S(1)}, u32[]{:S(2)}, u32[]{:S(2)}) %collective-permute-start.10) | collective-permute-done | bytes 262176 | tf_op jit(solution)/shard_map/ppermute | solution.py:228
  40.0 0.1 add_convert_fusion.1
  40.1 2.7 %collective-permute-start.11 = (bf16[2,64,1024]{2,1,0:T(8,128)(2,1)S(1)}, bf16[2,64,1024]{2,1,0:T(8,128)(2,1)S(1)}, u32[]{:S(2)}, u32[]{:S(2)}) collective-permute-start(bf16[2,64,1024]{2,1,0:T(8,128)(2,1)S(1)} %add_convert_fusion.1), channel_id=1, source_target_pairs={{0,4},{1,5},{2,6},{3,7},{4,0},{5,1},{6,2},{7,3},{8,12},{9,13},{10,... | collective-permute-start | bytes 786440 | tf_op jit(solution)/shard_map/ppermute | solution.py:228
  42.8 1.1 %shard_map.117.far = bf16[3,192,256]{2,1,0:T(8,128)(2,1)S(1)} custom-call(bf16[192,1024]{1,0:T(8,128)(2,1)S(1)} %bitcast.25, bf16[192,1024]{1,0:T(8,128)(2,1)S(1)} %bitcast.29, bf16[192,1024]{1,0:T(8,128)(2,1)S(1)} %bitcast.33, bf16[16,192,192]{2,1,0:T(8,128)(2,1)S(1)} %get-tuple-element.29.probs, bf16[192,1024]{1,0:T(8,128)(2,1)S(1)} %bitcast.22, ...), custom_call_target="tpu_custom_call" | custom-call | flops 301989888 | bytes 1048576 | tf_op jit(solution)/shard_map/pallas_call | solution.py:231
  43.8 0.0 collective-permute-done.13.d_near
  43.9 0.0 collective-permute-done.14.d_far
  43.9 2.1 %shard_map.118 = (bf16[192,1024]{1,0:T(8,128)(2,1)}, bf16[192,1024]{1,0:T(8,128)(2,1)}, bf16[192,1024]{1,0:T(8,128)(2,1)}) custom-call(bf16[192,1024]{1,0:T(8,128)(2,1)S(1)} %bitcast.26, bf16[192,1024]{1,0:T(8,128)(2,1)S(1)} %bitcast.30, bf16[192,1024]{1,0:T(8,128)(2,1)S(1)} %bitcast.34, bf16[16,192,192]{2,1,0:T(8,128)(2,1)S(1)} %get-tuple-element.29.probs, ...), custom_call_target="tpu_custom_call" | custom-call | flops 603979776 | bytes 1048576 | tf_op jit(solution)/shard_map/pallas_call | solution.py:231
  46.0 0.0 collective-permute-done.7
  46.0 0.3 add_convert_fusion.branches
  46.3 0.0 copy-start.4
  46.3 0.6 %collective-permute-start.8 = (bf16[192,1024]{1,0:T(8,128)(2,1)S(1)}, bf16[192,1024]{1,0:T(8,128)(2,1)S(1)}, u32[]{:S(2)}, u32[]{:S(2)}) collective-permute-start(bf16[192,1024]{1,0:T(8,128)(2,1)S(1)} %slice.15), channel_id=1, source_target_pairs={{0,2},{1,3},{2,0},{3,1},{4,6},{5,7},{6,4},{7,5},{8,10},{9,11},{10,... | collective-permute-start | bytes 1179656 | tf_op jit(solution)/shard_map/ppermute | solution.py:228
  47.0 0.0 collective-permute-done.9
  47.0 1.5 %collective-permute-done.11 = bf16[2,64,1024]{2,1,0:T(8,128)(2,1)S(1)} collective-permute-done((bf16[2,64,1024]{2,1,0:T(8,128)(2,1)S(1)}, bf16[2,64,1024]{2,1,0:T(8,128)(2,1)S(1)}, u32[]{:S(2)}, u32[]{:S(2)}) %collective-permute-start.11) | collective-permute-done | bytes 262176 | tf_op jit(solution)/shard_map/ppermute | solution.py:228
  48.5 0.1 convert_add_fusion
  48.6 3.2 %collective-permute-start.12 = (bf16[1,64,1024]{2,1,0:T(8,128)(2,1)S(1)}, bf16[1,64,1024]{2,1,0:T(8,128)(2,1)S(1)}, u32[]{:S(2)}, u32[]{:S(2)}) collective-permute-start(bf16[1,64,1024]{2,1,0:T(8,128)(2,1)S(1)} %slice.20), channel_id=1, source_target_pairs={{0,8},{1,9},{2,10},{3,11},{4,12},{5,13},{6,14},{7,15},{8,0},{9,1},... | collective-permute-start | bytes 393224 | tf_op jit(solution)/shard_map/ppermute | solution.py:228
  51.8 4.3 %collective-permute-done.12 = bf16[1,64,1024]{2,1,0:T(8,128)(2,1)S(1)} collective-permute-done((bf16[1,64,1024]{2,1,0:T(8,128)(2,1)S(1)}, bf16[1,64,1024]{2,1,0:T(8,128)(2,1)S(1)}, u32[]{:S(2)}, u32[]{:S(2)}) %collective-permute-start.12) | collective-permute-done | bytes 131104 | tf_op jit(solution)/shard_map/ppermute | solution.py:228
  56.1 0.9 %shard_map.115 = (bf16[192,1024]{1,0:T(8,128)(2,1)}, f32[64,1024]{1,0:T(8,128)}) custom-call(bf16[192,1024]{1,0:T(8,128)(2,1)S(1)} %bitcast.35, bf16[192,2048]{1,0:T(8,128)(2,1)S(1)} %add_convert_fusion.branches, bf16[192,1024]{1,0:T(8,128)(2,1)S(1)} %collective-permute-done.8.other, f32[64,1024]{1,0:T(8,128)S(1)} %slice_bitcast_fusion.kept, ...), custom_call_target="tpu_custom_call" | custom-call | flops 1048576 | bytes 1048576 | tf_op jit(solution)/shard_map/pallas_call | solution.py:231
  (11 shorter events, 0.1 us)
Async XLA Ops:
  0.6 10.6 %collective-permute-start = (bf16[1,64,1024]{2,1,0:T(8,128)(2,1)}, bf16[1,64,1024]{2,1,0:T(8,128)(2,1)S(1)}, u32[]{:S(2)}, u32[]{:S(2)}) collective-permute-start(bf16[1,64,1024]{2,1,0:T(8,128)(2,1)} %param.10), channel_id=1, source_target_pairs={{0,8},{1,9},{2,10},{3,11},{4,12},{5,13},{6,14},{7,15},{8,0},{9,1},... | collective-permute-start | bytes 393224 | tf_op jit(solution)/shard_map/ppermute | solution.py:228
  12.2 7.5 %collective-permute-start.1 = (bf16[2,64,1024]{2,1,0:T(8,128)(2,1)S(1)}, bf16[2,64,1024]{2,1,0:T(8,128)(2,1)S(1)}, u32[]{:S(2)}, u32[]{:S(2)}) collective-permute-start(bf16[2,64,1024]{2,1,0:T(8,128)(2,1)S(1)} %maximum_bitcast_fusion.near.rows), channel_id=1, source_target_pairs={{0,1},{1,0},{2,3},{3,2},{4,5},{5,4},{6,7},{7,6},{8,9},{9,8},{10,11... | collective-permute-start | bytes 786440 | tf_op jit(solution)/shard_map/ppermute | solution.py:228
  14.8 6.6 %copy-start.1 = (bf16[1,1,192,1024]{3,2,1,0:T(8,128)(2,1)S(1)}, bf16[1,1,192,1024]{3,2,1,0:T(8,128)(2,1)}, u32[]{:S(2)}) copy-start(bf16[1,1,192,1024]{3,2,1,0:T(8,128)(2,1)} %param.7) | copy-start | bytes 1179652
  14.8 6.6 %copy-start.2 = (bf16[1,1,192,1024]{3,2,1,0:T(8,128)(2,1)S(1)}, bf16[1,1,192,1024]{3,2,1,0:T(8,128)(2,1)}, u32[]{:S(2)}) copy-start(bf16[1,1,192,1024]{3,2,1,0:T(8,128)(2,1)} %param.8) | copy-start | bytes 1179652
  14.8 6.6 %copy-start.3 = (bf16[1,1,192,1024]{3,2,1,0:T(8,128)(2,1)S(1)}, bf16[1,1,192,1024]{3,2,1,0:T(8,128)(2,1)}, u32[]{:S(2)}) copy-start(bf16[1,1,192,1024]{3,2,1,0:T(8,128)(2,1)} %param.9) | copy-start | bytes 1179652
  14.8 6.6 %copy-start.5 = (s32[1,192]{1,0:T(1,128)S(1)}, s32[1,192]{1,0:T(1,128)}, u32[]{:S(2)}) copy-start(s32[1,192]{1,0:T(1,128)} %ids_ref.1) | copy-start | bytes 2308
  14.8 10.4 %collective-permute-start.5 = (bf16[96,1024]{1,0:T(8,128)(2,1)S(1)}, bf16[96,1024]{1,0:T(8,128)(2,1)S(1)}, u32[]{:S(2)}, u32[]{:S(2)}) collective-permute-start(bf16[96,1024]{1,0:T(8,128)(2,1)S(1)} %dynamic-slice_bitcast_fusion), channel_id=1, source_target_pairs={{0,2},{1,3},{2,0},{3,1},{4,6},{5,7},{6,4},{7,5},{8,10},{9,11},{10,... | collective-permute-start | bytes 589832 | tf_op jit(solution)/shard_map/ppermute | solution.py:228
  16.4 13.0 %collective-permute-start.2 = (bf16[2,64,1024]{2,1,0:T(8,128)(2,1)S(1)}, bf16[2,64,1024]{2,1,0:T(8,128)(2,1)S(1)}, u32[]{:S(2)}, u32[]{:S(2)}) collective-permute-start(bf16[2,64,1024]{2,1,0:T(8,128)(2,1)S(1)} %maximum_bitcast_fusion.near.rows), channel_id=1, source_target_pairs={{0,4},{1,5},{2,6},{3,7},{4,0},{5,1},{6,2},{7,3},{8,12},{9,13},{10,... | collective-permute-start | bytes 786440 | tf_op jit(solution)/shard_map/ppermute | solution.py:228
  19.7 9.6 %collective-permute-start.3 = (bf16[2,64,1024]{2,1,0:T(8,128)(2,1)S(1)}, bf16[2,64,1024]{2,1,0:T(8,128)(2,1)S(1)}, u32[]{:S(2)}, u32[]{:S(2)}) collective-permute-start(bf16[2,64,1024]{2,1,0:T(8,128)(2,1)S(1)} %collective-permute-done.1.near_x.rows_x), channel_id=1, source_target_pairs={{0,4},{1,5},{2,6},{3,7},{4,0},{5,1},{6,2},{7,3},{8,12},{9,13},{10,... | collective-permute-start | bytes 786440 | tf_op jit(solution)/shard_map/ppermute | solution.py:228
  23.6 8.1 %copy-start = (bf16[1,192,1024]{2,1,0:T(8,128)(2,1)S(1)}, bf16[1,192,1024]{2,1,0:T(8,128)(2,1)}, u32[]{:S(2)}) copy-start(bf16[1,192,1024]{2,1,0:T(8,128)(2,1)} %param.13) | copy-start | bytes 1179652
  23.6 5.8 %collective-permute-start.4 = (bf16[192,512]{1,0:T(8,128)(2,1)S(1)}, bf16[192,512]{1,0:T(8,128)(2,1)S(1)}, u32[]{:S(2)}, u32[]{:S(2)}) collective-permute-start(bf16[192,512]{1,0:T(8,128)(2,1)S(1)} %get-tuple-element.22), channel_id=1, source_target_pairs={{0,2},{1,3},{2,0},{3,1},{4,6},{5,7},{6,4},{7,5},{8,10},{9,11},{10,... | collective-permute-start | bytes 589832 | tf_op jit(solution)/shard_map/ppermute | solution.py:228
  25.2 4.2 %collective-permute-start.6 = (bf16[96,1024]{1,0:T(8,128)(2,1)S(1)}, bf16[96,1024]{1,0:T(8,128)(2,1)S(1)}, u32[]{:S(2)}, u32[]{:S(2)}) collective-permute-start(bf16[96,1024]{1,0:T(8,128)(2,1)S(1)} %collective-permute-done.5.rest_0_), channel_id=1, source_target_pairs={{0,16},{16,0},{1,17},{17,1},{2,18},{18,2},{3,19},{19,3},{4,20},{20... | collective-permute-start | bytes 589832 | tf_op jit(solution)/shard_map/ppermute | solution.py:260
  30.3 15.7 %collective-permute-start.7 = (bf16[192,2048]{1,0:T(8,128)(2,1)S(1)}, bf16[192,2048]{1,0:T(8,128)(2,1)S(1)}, u32[]{:S(2)}, u32[]{:S(2)}) collective-permute-start(bf16[192,2048]{1,0:T(8,128)(2,1)S(1)} %get-tuple-element.23), channel_id=1, source_target_pairs={{0,16},{1,17},{2,18},{3,19},{4,20},{5,21},{6,22},{7,23},{8,24},{9,... | collective-permute-start | bytes 2359304 | tf_op jit(solution)/shard_map/ppermute | solution.py:325
  32.3 7.7 %collective-permute-start.10 = (bf16[2,64,1024]{2,1,0:T(8,128)(2,1)S(1)}, bf16[2,64,1024]{2,1,0:T(8,128)(2,1)S(1)}, u32[]{:S(2)}, u32[]{:S(2)}) collective-permute-start(bf16[2,64,1024]{2,1,0:T(8,128)(2,1)S(1)} %get-tuple-element.27), channel_id=1, source_target_pairs={{0,1},{1,0},{2,3},{3,2},{4,5},{5,4},{6,7},{7,6},{8,9},{9,8},{10,11... | collective-permute-start | bytes 786440 | tf_op jit(solution)/shard_map/ppermute | solution.py:228
  35.2 8.6 %collective-permute-start.13 = (bf16[192,256]{1,0:T(8,128)(2,1)S(1)}, bf16[192,256]{1,0:T(8,128)(2,1)S(1)}, u32[]{:S(2)}, u32[]{:S(2)}) collective-permute-start(bf16[192,256]{1,0:T(8,128)(2,1)S(1)} %get-tuple-element.30), channel_id=1, source_target_pairs={{0,2},{1,3},{2,0},{3,1},{4,6},{5,7},{6,4},{7,5},{8,10},{9,11},{10,... | collective-permute-start | bytes 294920 | tf_op jit(solution)/shard_map/ppermute | solution.py:228
  37.4 9.5 %collective-permute-start.9 = (bf16[2,64,1024]{2,1,0:T(8,128)(2,1)S(1)}, bf16[2,64,1024]{2,1,0:T(8,128)(2,1)S(1)}, u32[]{:S(2)}, u32[]{:S(2)}) collective-permute-start(bf16[2,64,1024]{2,1,0:T(8,128)(2,1)S(1)} %get-tuple-element.25), channel_id=1, source_target_pairs={{0,1},{1,0},{2,3},{3,2},{4,5},{5,4},{6,7},{7,6},{8,9},{9,8},{10,11... | collective-permute-start | bytes 786440 | tf_op jit(solution)/shard_map/ppermute | solution.py:228
  38.1 5.8 %collective-permute-start.14 = (bf16[192,256]{1,0:T(8,128)(2,1)S(1)}, bf16[192,256]{1,0:T(8,128)(2,1)S(1)}, u32[]{:S(2)}, u32[]{:S(2)}) collective-permute-start(bf16[192,256]{1,0:T(8,128)(2,1)S(1)} %get-tuple-element.31), channel_id=1, source_target_pairs={{0,2},{1,3},{2,0},{3,1},{4,6},{5,7},{6,4},{7,5},{8,10},{9,11},{10,... | collective-permute-start | bytes 294920 | tf_op jit(solution)/shard_map/ppermute | solution.py:228
  40.1 8.4 %collective-permute-start.11 = (bf16[2,64,1024]{2,1,0:T(8,128)(2,1)S(1)}, bf16[2,64,1024]{2,1,0:T(8,128)(2,1)S(1)}, u32[]{:S(2)}, u32[]{:S(2)}) collective-permute-start(bf16[2,64,1024]{2,1,0:T(8,128)(2,1)S(1)} %add_convert_fusion.1), channel_id=1, source_target_pairs={{0,4},{1,5},{2,6},{3,7},{4,0},{5,1},{6,2},{7,3},{8,12},{9,13},{10,... | collective-permute-start | bytes 786440 | tf_op jit(solution)/shard_map/ppermute | solution.py:228
  46.3 9.8 %copy-start.4 = (bf16[1,192,1024]{2,1,0:T(8,128)(2,1)S(1)}, bf16[1,192,1024]{2,1,0:T(8,128)(2,1)}, u32[]{:S(2)}) copy-start(bf16[1,192,1024]{2,1,0:T(8,128)(2,1)} %param.12) | copy-start | bytes 1179652
  46.3 9.8 %collective-permute-start.8 = (bf16[192,1024]{1,0:T(8,128)(2,1)S(1)}, bf16[192,1024]{1,0:T(8,128)(2,1)S(1)}, u32[]{:S(2)}, u32[]{:S(2)}) collective-permute-start(bf16[192,1024]{1,0:T(8,128)(2,1)S(1)} %slice.15), channel_id=1, source_target_pairs={{0,2},{1,3},{2,0},{3,1},{4,6},{5,7},{6,4},{7,5},{8,10},{9,11},{10,... | collective-permute-start | bytes 1179656 | tf_op jit(solution)/shard_map/ppermute | solution.py:228
  48.6 7.5 %collective-permute-start.12 = (bf16[1,64,1024]{2,1,0:T(8,128)(2,1)S(1)}, bf16[1,64,1024]{2,1,0:T(8,128)(2,1)S(1)}, u32[]{:S(2)}, u32[]{:S(2)}) collective-permute-start(bf16[1,64,1024]{2,1,0:T(8,128)(2,1)S(1)} %slice.20), channel_id=1, source_target_pairs={{0,8},{1,9},{2,10},{3,11},{4,12},{5,13},{6,14},{7,15},{8,0},{9,1},... | collective-permute-start | bytes 393224 | tf_op jit(solution)/shard_map/ppermute | solution.py:228
